TPU v7x, 256 devices: a whole 4x4x8 slice. The times are simulated.
256 devices in a mesh: dp: 32 (over x, z), mp: 8 (over y, core).
Axes of the slice: x: 4, y: 4, z: 8, core: 2. Of those that a mesh axis runs over, the one named last changes fastest.
Arguments:
- query_emb: bfloat16 [8192, 768], P('dp'), may hold values from -6 to 6
- positive_list: int32 [8192], replicated, may hold values from 0 to 32767
- centroids: float32 [32768, 768], P(('dp', 'mp')), may hold values from -0.6 to 0.6
- first_moment: float32 [32768, 768], P(('dp', 'mp')), may hold values from -3 to 3
- second_moment: float32 [32768, 768], P(('dp', 'mp')), may hold values from 0.05 to 2
Outputs:
- new_centroids: float32 [32768, 768], P(('dp', 'mp'))
- new_first: float32 [32768, 768], P(('dp', 'mp'))
- new_second: float32 [32768, 768], P(('dp', 'mp'))
- mean_loss: float32 [], replicated
All inputs are finite; a program needn't handle non-finite values.
Results may differ from a plain program's by a relative error of at most 0.00097.
Values may be sent and summed in bfloat16 or wider, within the bound.
A program may use at most 64 MiB of HBM per device.

v0:
```python
import jax
import jax.numpy as jnp
from jax import lax
from jax.sharding import Mesh
from jax.sharding import PartitionSpec as P

MP = ("mp_0", "mp_1")
DP = ("dp_0", "dp_1")
DP_MP = ("dp_0", "dp_1", "mp_0", "mp_1")


beta_first = 0.9
beta_second = 0.95
learn_rate = 0.01
epsilon = 1e-08


def all_in_one(x, axis):
    leaves = jax.tree.leaves(x)
    turns = sorted(range(len(leaves)), key=lambda k: -leaves[k].size)
    width = (1, *leaves[turns[0]].shape)[-1]
    lines = [
        jnp.pad(leaves[k].reshape(-1), (0, -leaves[k].size % width)).reshape(-1, width)
        for k in turns
    ]
    both, at, found = (lax.all_gather(jnp.concatenate(lines), axis), 0, {})
    for k, line in zip(turns, lines):
        piece = both[:, at : at + len(line)].reshape(len(both), -1)
        found[k] = piece[:, : leaves[k].size].reshape(-1, *leaves[k].shape)
        at += len(line)
    numbers = iter(range(len(leaves)))
    return jax.tree.map(lambda _: found[next(numbers)], x)


def combined_by_axis(x, axes, combine):
    for axis in axes:
        pieces = all_in_one(x, axis)
        x = jax.tree.map(lambda part: part[0], pieces)
        for k in range(1, lax.axis_size(axis)):
            x = combine(x, jax.tree.map(lambda part: part[k], pieces))
    return x


def adam_update(centroids, first_moment, second_moment, gradient):
    new_first = beta_first * first_moment + (1.0 - beta_first) * gradient
    new_second = beta_second * second_moment + (1.0 - beta_second) * gradient * gradient
    new_centroids = centroids - learn_rate * new_first / (jnp.sqrt(new_second) + epsilon)
    return (new_centroids, new_first, new_second)


def combine(left_part, right_part):
    top_value = jnp.maximum(left_part[0], right_part[0])
    summed = left_part[1] * jnp.exp(left_part[0] - top_value) + right_part[1] * jnp.exp(
        right_part[0] - top_value
    )
    return (top_value, summed, left_part[2] + right_part[2])


def target_logit(logits, is_target):
    return jnp.sum(jnp.where(is_target, logits, jnp.zeros_like(logits)), axis=1)


def row_terms(logits, is_target, row_peak, row_mass, row_target):
    log_norm = row_peak + jnp.log(row_mass)
    row_loss = log_norm - row_target
    weights = (jnp.exp(logits - log_norm[:, None]) - is_target.astype(jnp.float32)).astype(
        jnp.bfloat16
    )
    return (row_loss, weights)


def shards(query_emb, positive_list, centroids, first_moment, second_moment):
    table_half = centroids.astype(jnp.bfloat16)
    own_lists = centroids.shape[0]
    count_mp = lax.axis_size(MP)
    dp_index = lax.axis_index(DP)
    mp_index = lax.axis_index(MP)
    gathered = lax.all_gather(query_emb, DP, axis=0, tiled=True)
    logits = jnp.einsum("rd,kd->rk", gathered, table_half, preferred_element_type=jnp.float32)
    shard_block = dp_index * count_mp + mp_index
    global_col = shard_block * own_lists + lax.iota(jnp.int32, own_lists)
    is_target = global_col[None, :] == positive_list[:, None]
    local_peak = jnp.max(logits, axis=1)
    local_mass = jnp.sum(jnp.exp(logits - local_peak[:, None]), axis=1)
    row_peak, row_mass, row_target = combined_by_axis(
        (local_peak, local_mass, target_logit(logits, is_target)), DP_MP, combine
    )
    row_loss, weights = row_terms(logits, is_target, row_peak, row_mass, row_target)
    mean_loss = jnp.mean(row_loss)
    gradient = jnp.einsum("rk,rd->kd", weights, gathered, preferred_element_type=jnp.float32)
    new_centroids, new_first, new_second = adam_update(
        centroids, first_moment, second_moment, gradient
    )
    return (new_centroids, new_first, new_second, mean_loss)


def solution(mesh):
    split = Mesh(mesh.devices.reshape(4, 8, 4, 2), ("dp_0", "dp_1", "mp_0", "mp_1"))
    placed = (P(DP, None), P(), P(DP_MP, None), P(DP_MP, None), P(DP_MP, None))
    return jax.shard_map(
        shards,
        mesh=split,
        in_specs=placed,
        out_specs=(P(DP_MP, None), P(DP_MP, None), P(DP_MP, None), P()),
        check_vma=False,
    )
```

profile of v0, /device:TPU:1, one launch (start us, length us, event | category | flops | bytes accessed | tf_op | source)
XLA Modules:
  0.0 219.7 jit_solution(9997302614362853183)
XLA Ops:
  7.2 0.0 all-gather.10.cloned.1.call-start
  7.2 0.7 all-gather.10.cloned.1.call-update
  7.9 0.0 copy-start.4
  7.9 124.4 %all-gather.10.cloned.1.call-done = bf16[8192,768]{1,0:T(8,128)(2,1)} async-done(((bf16[256,768]{1,0:T(8,128)(2,1)}), bf16[8192,768]{1,0:T(8,128)(2,1)}) %all-gather.10.cloned.1.call-update) | async-done | bytes 12582928 | tf_op jit(solution)/shard_map/all_gather | solution.py:78
  132.3 8.7 %fusion.73 = (f32[8192]{0:T(1024)S(1)}, f32[8192,128]{0,1:T(8,128)S(1)}) fusion(bf16[8192,768]{1,0:T(8,128)(2,1)} %all-gather.10.cloned.1.call-done, f32[128,768]{1,0:T(8,128)} %param.7), kind=kOutput, calls=%fused_computation.128 | convolution fusion | flops 1611751424 | bytes 17203200 | tf_op jit(solution)/shard_map/rd,kd->rk/dot_general | solution.py:79
  141.0 0.0 copy-start
  141.0 0.0 copy-done.4
  141.1 1.1 exponential_reduce_fusion
  142.1 0.0 copy-start.1
  142.1 0.0 copy-start.2
  142.1 0.0 copy-start.3
  142.2 0.1 maximum_bitcast_fusion
  142.3 10.2 %all-gather.4 = f32[4,3,8192]{2,1,0:T(4,128)S(1)} all-gather(f32[1,3,8192]{2,1,0:T(4,128)S(1)} %maximum_bitcast_fusion), channel_id=2, replica_groups=mesh['dp_0'=4,'dp_1'=8,'mp_0'=4,'mp_1'=2] {'dp_0'}, dimensions={0}, use_global_device_ids=true | all-gather | bytes 491520 | tf_op jit(solution)/shard_map/all_gather | solution.py:26
  152.5 0.1 fusion.43
  152.6 0.3 fusion.45
  153.0 0.1 maximum_bitcast_fusion.1
  153.1 21.0 %all-gather.5 = f32[8,3,8192]{2,1,0:T(4,128)S(1)} all-gather(f32[1,3,8192]{2,1,0:T(4,128)S(1)} %maximum_bitcast_fusion.1), channel_id=3, replica_groups=mesh['dp_0'=4,'dp_1'=8,'mp_0'=4,'mp_1'=2] {'dp_1'}, dimensions={0}, use_global_device_ids=true | all-gather | bytes 884736 | tf_op jit(solution)/shard_map/all_gather | solution.py:26
  174.0 0.2 fusion.21
  174.2 0.7 fusion.23
  175.0 0.1 maximum_bitcast_fusion.2
  175.1 10.5 %all-gather.6 = f32[4,3,8192]{2,1,0:T(4,128)S(1)} all-gather(f32[1,3,8192]{2,1,0:T(4,128)S(1)} %maximum_bitcast_fusion.2), channel_id=4, replica_groups=mesh['dp_0'=4,'dp_1'=8,'mp_0'=4,'mp_1'=2] {'mp_0'}, dimensions={0}, use_global_device_ids=true | all-gather | bytes 491520 | tf_op jit(solution)/shard_map/all_gather | solution.py:26
  185.6 0.0 copy-done
  185.6 0.1 fusion.11
  185.7 0.3 fusion.13
  186.1 0.1 maximum_bitcast_fusion.3
  186.2 14.9 %all-gather.7 = f32[2,3,8192]{2,1,0:T(4,128)S(1)} all-gather(f32[1,3,8192]{2,1,0:T(4,128)S(1)} %maximum_bitcast_fusion.3), channel_id=5, replica_groups=mesh['dp_0'=4,'dp_1'=8,'mp_0'=4,'mp_1'=2] {'mp_1'}, dimensions={0}, use_global_device_ids=true | all-gather | bytes 294912 | tf_op jit(solution)/shard_map/all_gather | solution.py:26
  201.1 0.1 fusion.72
  201.2 0.6 subtract_reduce_fusion
  202.5 0.0 copy-done.1
  202.5 0.0 copy-done.2
  202.5 0.0 copy-done.3
  202.5 9.2 %divide_subtract_fusion = (f32[128,768]{1,0:T(8,128)}, f32[128,768]{1,0:T(8,128)}, f32[128,768]{1,0:T(8,128)}) fusion(f32[128,768]{1,0:T(8,128)S(1)} %copy-done.1, f32[128,768]{1,0:T(8,128)S(1)} %copy-done.2, f32[128,768]{1,0:T(8,128)S(1)} %copy-done.3, bf16[8192,768]{1,0:T(8,128)(2,1)} %all-gather.10.cloned.1.call-done, f32[8192,128]{0,1:T(8,128)} %copy-done, ...), kind=kOutput, calls=%fused_computation.12 | convolution fusion | flops 1616936960 | bytes 19202560 | tf_op jit(solution)/shard_map/rk,rd->kd/dot_general | solution.py:90
  (1 shorter events, 0.0 us)
Async XLA Ops:
  7.2 125.2 %all-gather.10.cloned.1.call-start = ((), (), s32[]{:S(2)}) async-start(), calls=%async_computation | async-start | bytes 12976128 | tf_op jit(solution)/shard_map/all_gather | solution.py:78
  7.9 133.1 %copy-start.4 = (s32[8192]{0:T(1024)S(1)}, s32[8192]{0:T(1024)}, u32[]{:S(2)}) copy-start(s32[8192]{0:T(1024)} %param.6) | copy-start | bytes 98308
  141.0 44.6 %copy-start = (f32[8192,128]{0,1:T(8,128)}, f32[8192,128]{0,1:T(8,128)S(1)}, u32[]{:S(2)}) copy-start(f32[8192,128]{0,1:T(8,128)S(1)} %get-tuple-element.23) | copy-start | bytes 12582916
  142.1 60.4 %copy-start.1 = (f32[128,768]{1,0:T(8,128)S(1)}, f32[128,768]{1,0:T(8,128)}, u32[]{:S(2)}) copy-start(f32[128,768]{1,0:T(8,128)} %param.7) | copy-start | bytes 1179652
  142.1 60.4 %copy-start.2 = (f32[128,768]{1,0:T(8,128)S(1)}, f32[128,768]{1,0:T(8,128)}, u32[]{:S(2)}) copy-start(f32[128,768]{1,0:T(8,128)} %param.8) | copy-start | bytes 1179652
  142.1 60.4 %copy-start.3 = (f32[128,768]{1,0:T(8,128)S(1)}, f32[128,768]{1,0:T(8,128)}, u32[]{:S(2)}) copy-start(f32[128,768]{1,0:T(8,128)} %param.9) | copy-start | bytes 1179652
Sparse Core Ops, SparseCore 0:
  10.6 121.7 all-gather.9
where the time goes:
time: 220 us
  waiting for transfers between devices  125 us (57%)
  blocking collectives  56.6 us (26%)
  matrix products  17.9 us (8%)
  between operations  16 us (7%)
  other arithmetic  4.04 us (2%)
    all_gather x1, waiting for transfers between devices, shards(): gathered = lax.all_gather(query_emb, DP, axis=0, tiled=True)  124 us
    all_gather x4, blocking collectives, all_in_one(): both, at, found = (lax.all_gather(jnp.concatenate(lines), axis), 0, {})  56.6 us
    dot_general x1, matrix products, shards(): jnp.einsum('rk,rd->kd', weights, gathered, preferred_element_type=jnp.flo...  9.24 us
    dot_general x1, matrix products, shards(): jnp.einsum('rd,kd->rk', gathered, table_half, preferred_element_type=jnp....  8.7 us
  transfers between devices with their start and end apart: 1, of which 1 were waited for; matrix products, arithmetic and copies ran while one was open for 0% of the time, Pallas kernels for 0%

commit v1 on v0

v1 whole, which is shorter than its diff:
```python
import jax
import jax.numpy as jnp
from jax import lax
from jax.experimental import pallas as pl
from jax.experimental.pallas import tpu as pltpu
from jax.sharding import Mesh
from jax.sharding import PartitionSpec as P

NX, NZ, NY, NC = 4, 8, 4, 2
AXES = ("x", "z", "y", "c")
DP = ("x", "z")
DP_MP = ("x", "z", "y", "c")
MESH = pl.DeviceIdType.MESH

ROWS = 8192
D = 768
LISTS = 32768
BLOCKS = NX * NZ
CLASSES = 4
BLOCK_ROWS = ROWS // BLOCKS // CLASSES
DEV_ROWS = BLOCKS * BLOCK_ROWS
OWN = LISTS // (NX * NZ * NY * NC)
HELD = 4 * OWN
TILES = DEV_ROWS // 128
GROUP = 4 * BLOCK_ROWS
SENDS = 31
PARTS = 4

beta_first = 0.9
beta_second = 0.95
learn_rate = 0.01
epsilon = 1e-08


def adam_update(centroids, first_moment, second_moment, gradient):
    new_first = beta_first * first_moment + (1.0 - beta_first) * gradient
    new_second = beta_second * second_moment + (1.0 - beta_second) * gradient * gradient
    new_centroids = centroids - learn_rate * new_first / (jnp.sqrt(new_second) + epsilon)
    return (new_centroids, new_first, new_second)


def log_sum_exp(slots):
    top = slots[0]
    for part in slots[1:]:
        top = jnp.maximum(top, part)
    total = jnp.exp(slots[0] - top)
    for part in slots[1:]:
        total = total + jnp.exp(part - top)
    return top + jnp.log(total)


def kernel(
    query_hbm, pos_ref, cent_ref, grad_ref, loss_ref,
    q, table, logits, weights, norm, stat1, stat2, loss1, loss2, loss3, part, from_partner, y_out, y_in,
    own_sem, q_send, q_recv, t_send, t_recv,
    s1_send, s1_recv, s2_send, s2_recv, l1_send, l1_recv, l2_send, l2_recv, l3_send, l3_recv,
    d_send, d_recv, y_send, y_recv,
):
    x, z, y, c = (lax.axis_index(a) for a in AXES)
    turn = 1 - 2 * c

    def at_x(k):
        return lax.rem(x + (k + NX), NX)

    def at_z(k):
        return lax.rem(z + (k + NZ), NZ)

    def at_y(k):
        return lax.rem(y + (k + NY), NY)

    helper_y = at_y(turn)
    owner_y = at_y(-turn)
    other = 1 - c

    def remote(src, dst, send, recv, where):
        copy = pltpu.make_async_remote_copy(
            src_ref=src, dst_ref=dst, send_sem=send, recv_sem=recv, device_id=where, device_id_type=MESH
        )
        copy.start()
        return copy

    def arrived(dst, sem):
        pltpu.make_async_copy(dst, dst, sem).wait()

    row_class = lax.rem(y, 2) * 2 + c
    own_place = jnp.where(c == 0, z * NX + x, x * NZ + z)
    own_copy = pltpu.make_async_copy(
        query_hbm.at[pl.ds(pl.multiple_of(row_class * BLOCK_ROWS, BLOCK_ROWS), BLOCK_ROWS)], q.at[own_place], own_sem
    )
    own_copy.start()
    table[0] = cent_ref[...].astype(jnp.bfloat16)

    group1 = [(dx, dy) for dy in (0, 2) for dx in range(NX) if (dx, dy) != (0, 0)]
    peers = [{"x": at_x(dx), "y": at_y(dy)} for dx, dy in group1]
    peers += [{"z": at_z(dz)} for dz in range(1, NZ)]
    peers += [{"y": at_y(1)}, {"y": at_y(-1)}, {"c": other}, {"y": helper_y, "c": other}]
    barrier = pltpu.get_barrier_semaphore()
    for peer in peers:
        pl.semaphore_signal(barrier, inc=1, device_id=peer, device_id_type=MESH)
    pl.semaphore_wait(barrier, len(peers))

    own_copy.wait()

    table_sends = [
        remote(table.at[0], table.at[1], t_send.at[0], t_recv.at[0], {"y": helper_y}),
        remote(table.at[0], table.at[2], t_send.at[1], t_recv.at[1], {"c": other}),
        remote(table.at[0], table.at[3], t_send.at[2], t_recv.at[2], {"y": helper_y, "c": other}),
    ]

    right, left = {"x": at_x(1)}, {"x": at_x(-1)}
    up, down = {"z": at_z(1)}, {"z": at_z(-1)}

    def passes(place_of):
        count = [0]

        def send(bx, bz, where):
            place = place_of(bx, bz)
            k = count[0]
            count[0] += 1
            remote(q.at[place], q.at[place], q_send.at[k], q_recv.at[place], where)

        def take(bx, bz):
            place = place_of(bx, bz)
            arrived(q.at[place], q_recv.at[place])

        return send, take, count

    send_a, take_a, count_a = passes(lambda bx, bz: bz * NX + bx)
    columns = (0, -1, 1, 2)

    def round_a(r):
        if r == 0:
            send_a(x, z, right)
            send_a(x, z, left)
            send_a(x, z, up)
            send_a(x, z, down)
            take_a(at_x(-1), z)
            send_a(at_x(-1), z, right)
            send_a(at_x(-1), z, up)
            send_a(at_x(-1), z, down)
            take_a(at_x(1), z)
            send_a(at_x(1), z, up)
            send_a(at_x(1), z, down)
            take_a(at_x(2), z)
            send_a(at_x(2), z, up)
            send_a(at_x(2), z, down)
        elif r in (1, 3, 5):
            s = (r + 1) // 2
            for j, k in enumerate(columns):
                bx = at_x(k)
                take_a(bx, at_z(-s))
                if s < 3 or j < 2:
                    send_a(bx, at_z(-s), up)
                take_a(bx, at_z(s))
                if s < 3 or j >= 2:
                    send_a(bx, at_z(s), down)
        elif r == 7:
            for k in columns:
                take_a(at_x(k), at_z(4))

    def place_a(r):
        s = (r + 1) // 2
        return at_z(-s if r % 2 else s) * GROUP

    send_b, take_b, count_b = passes(lambda bx, bz: bx * NZ + bz)
    along = (0, -1, 1, -2, 2, -3, 3, 4)

    def round_b(r):
        if r == 0:
            send_b(x, z, up)
            send_b(x, z, down)
            send_b(x, z, right)
            send_b(x, z, left)
            for k in along[1:]:
                take_b(x, at_z(k))
                if -4 < k < 0:
                    send_b(x, at_z(k), up)
                elif 0 < k < 3:
                    send_b(x, at_z(k), down)
                send_b(x, at_z(k), right)
                send_b(x, at_z(k), left)
        elif r == 2:
            for t, k in enumerate(along):
                take_b(at_x(-1), at_z(k))
                if t % 2 == 0:
                    send_b(at_x(-1), at_z(k), right)
                take_b(at_x(1), at_z(k))
                if t % 2 == 1:
                    send_b(at_x(1), at_z(k), left)
        elif r == 6:
            for k in along:
                take_b(at_x(2), at_z(k))

    def place_b(r):
        return at_x((0, -1, 1, 2)[r // 2]) * 2 * GROUP + (r % 2) * GROUP

    def move(r):
        @pl.when(c == 0)
        def _():
            round_a(r)

        @pl.when(c == 1)
        def _():
            round_b(r)

    def group_logits(r):
        start = pl.multiple_of(jnp.where(c == 0, place_a(r), place_b(r)), GROUP)
        rows = q[pl.ds(start // BLOCK_ROWS, 4)].reshape(GROUP, D)
        block = lax.dot_general(
            table[...].reshape(HELD, D), rows, (((1,), (1,)), ((), ())), preferred_element_type=jnp.float32
        )
        logits[:, pl.ds(start, GROUP)] = block
        peak = jnp.max(block, axis=0, keepdims=True)
        mass = jnp.sum(jnp.exp(block - peak), axis=0, keepdims=True)
        local = peak + jnp.log(mass)
        tile = start // 128
        norm[pl.ds(tile, 1), :] = local[:, :128]
        norm[pl.ds(tile + 1, 1), :] = local[:, 128:]

    move(0)
    move(1)
    for k in range(3):
        arrived(table.at[k + 1], t_recv.at[k])
    for r in range(8):
        group_logits(r)
        if r < 6:
            move(r + 2)
    assert count_a[0] == SENDS and count_b[0] == SENDS

    me1 = lax.div(y, 2) * NX + x

    def exchange1(slots, send, recv):
        for k, (dx, dy) in enumerate(group1):
            remote(slots.at[me1], slots.at[me1], send.at[k], recv.at[me1], {"x": at_x(dx), "y": at_y(dy)})

    def wait1(slots, send, recv):
        for k, (dx, dy) in enumerate(group1):
            place = lax.div(at_y(dy), 2) * NX + at_x(dx)
            arrived(slots.at[place], recv.at[place])
            arrived(slots.at[0], send.at[k])

    def exchange2(slots, send, recv):
        for dz in range(1, NZ):
            remote(slots.at[z], slots.at[z], send.at[dz - 1], recv.at[z], {"z": at_z(dz)})

    def wait2(slots, send, recv):
        for dz in range(1, NZ):
            arrived(slots.at[at_z(dz)], recv.at[at_z(dz)])
            arrived(slots.at[0], send.at[dz - 1])

    stat1[me1] = norm[...]
    exchange1(stat1, s1_send, s1_recv)
    wait1(stat1, s1_send, s1_recv)
    stat2[z] = log_sum_exp([stat1[k] for k in range(8)])
    exchange2(stat2, s2_send, s2_recv)
    wait2(stat2, s2_send, s2_recv)
    norm[...] = log_sum_exp([stat2[k] for k in range(8)])

    parity = lax.rem(y, 2)
    lane = lax.broadcasted_iota(jnp.int32, (1, 128), 1)
    sub = lax.broadcasted_iota(jnp.int32, (OWN, 128), 0)
    first_block = (x * NZ + z) * NY * NC
    held = [(y, c), (owner_y, c), (y, other), (helper_y, other)]
    ids = [sub + (first_block + hy * NC + hc) * OWN for hy, hc in held]

    def targets(b):
        return pos_ref[pl.ds(b * 2 + parity, 1), :]

    def tile_weights(j, loss):
        start = pl.multiple_of(j * 128, 128)
        even, odd = 2 * j, 2 * j + 1
        b0 = jnp.where(c == 0, lax.rem(even, NX) * NZ + lax.div(even, NX), even)
        b1 = jnp.where(c == 0, lax.rem(odd, NX) * NZ + lax.div(odd, NX), odd)
        r0, r1 = targets(b0), targets(b1)
        low = jnp.where(c == 0, r0, pltpu.roll(r0, 64, 1))
        high = jnp.where(c == 0, pltpu.roll(r1, 64, 1), r1)
        chosen = jnp.where(lane < 64, low, high)
        log_norm = norm[pl.ds(j, 1), :]
        for k in range(4):
            gap = logits[pl.ds(k * OWN, OWN), pl.ds(start, 128)] - log_norm
            is_target = ids[k] == chosen
            soft = jnp.exp(gap)
            weights[pl.ds(k * OWN, OWN), pl.ds(start, 128)] = jnp.where(is_target, soft - 1.0, soft).astype(
                jnp.bfloat16
            )
            missed = jnp.where(is_target, gap, 0.0)
            loss = loss - jnp.sum(missed.reshape(OWN // 8, 8, 128), axis=0)
        return loss

    loss = lax.fori_loop(0, TILES, tile_weights, jnp.zeros((8, 128), jnp.float32))
    loss1[me1] = loss
    exchange1(loss1, l1_send, l1_recv)

    def pair_gradient(first):
        def columns_of(n, carry):
            cols = pl.ds(pl.multiple_of(n * 256, 256), 256)
            part[pl.ds(first * OWN, 2 * OWN), cols] = jnp.dot(
                weights[pl.ds(first * OWN, 2 * OWN), :],
                q[:, :, cols].reshape(DEV_ROWS, 256),
                preferred_element_type=jnp.float32,
            )
            return carry

        lax.fori_loop(0, D // 256, columns_of, 0)

    pair_gradient(2)
    partner = {"c": other}
    to_partner = [
        remote(part.at[pl.ds(3 * OWN, OWN)], from_partner.at[1], d_send.at[1], d_recv.at[1], partner),
        remote(part.at[pl.ds(2 * OWN, OWN)], from_partner.at[0], d_send.at[0], d_recv.at[0], partner),
    ]
    pair_gradient(0)
    arrived(from_partner.at[1], d_recv.at[1])
    size = OWN // PARTS
    to_owner = []
    for k in range(PARTS):
        y_out[k] = part[pl.ds(OWN + k * size, size), :] + from_partner[1, pl.ds(k * size, size), :]
        to_owner.append(remote(y_out.at[k], y_in.at[k], y_send.at[k], y_recv.at[k], {"y": owner_y}))

    wait1(loss1, l1_send, l1_recv)
    total = loss1[0]
    for k in range(1, 8):
        total = total + loss1[k]
    loss2[z] = total
    exchange2(loss2, l2_send, l2_recv)

    arrived(from_partner.at[0], d_recv.at[0])
    grad_ref[...] = part[pl.ds(0, OWN), :] + from_partner[0]

    wait2(loss2, l2_send, l2_recv)
    total = loss2[0]
    for k in range(1, 8):
        total = total + loss2[k]
    loss3[0] = total
    across = remote(loss3.at[0], loss3.at[1], l3_send.at[0], l3_recv.at[0], partner)
    across.wait()
    loss3[2] = loss3[0] + loss3[1]
    last = remote(loss3.at[2], loss3.at[3], l3_send.at[1], l3_recv.at[1], {"y": owner_y})
    for k in range(PARTS):
        arrived(y_in.at[k], y_recv.at[k])
        rows = pl.ds(k * size, size)
        grad_ref[rows, :] = grad_ref[rows, :] + y_in[k]
    last.wait()
    loss_ref[...] = jnp.sum(loss3[2] + loss3[3], keepdims=True) * (1.0 / ROWS)

    for k in range(SENDS):
        arrived(q.at[0], q_send.at[k])
    for copy in table_sends + to_partner + to_owner:
        copy.wait_send()


def shards(query_emb, positive_list, centroids, first_moment, second_moment):
    f32, bf16, dma = jnp.float32, jnp.bfloat16, pltpu.SemaphoreType.DMA
    vmem = pl.BlockSpec(memory_space=pltpu.VMEM)
    gradient, loss = pl.pallas_call(
        kernel,
        name="step",
        out_shape=(jax.ShapeDtypeStruct((OWN, D), f32), jax.ShapeDtypeStruct((1, 1), f32)),
        in_specs=[pl.BlockSpec(memory_space=pl.ANY), vmem, vmem],
        out_specs=(vmem, vmem),
        scratch_shapes=[
            pltpu.VMEM((BLOCKS, BLOCK_ROWS, D), bf16),
            pltpu.VMEM((4, OWN, D), bf16),
            pltpu.VMEM((HELD, DEV_ROWS), f32),
            pltpu.VMEM((HELD, DEV_ROWS), bf16),
            pltpu.VMEM((TILES, 128), f32),
            pltpu.VMEM((8, TILES, 128), f32),
            pltpu.VMEM((8, TILES, 128), f32),
            pltpu.VMEM((8, 8, 128), f32),
            pltpu.VMEM((8, 8, 128), f32),
            pltpu.VMEM((4, 8, 128), f32),
            pltpu.VMEM((HELD, D), f32),
            pltpu.VMEM((2, OWN, D), f32),
            pltpu.VMEM((PARTS, OWN // PARTS, D), f32),
            pltpu.VMEM((PARTS, OWN // PARTS, D), f32),
            dma, dma((SENDS,)), dma((BLOCKS,)), dma((3,)), dma((3,)),
            dma((7,)), dma((8,)), dma((7,)), dma((8,)), dma((7,)), dma((8,)), dma((7,)), dma((8,)), dma((2,)), dma((2,)),
            dma((2,)), dma((2,)), dma((PARTS,)), dma((PARTS,)),
        ],
        compiler_params=pltpu.CompilerParams(
            collective_id=0, has_side_effects=True, vmem_limit_bytes=48 * 1024 * 1024
        ),
    )(query_emb, positive_list.reshape(ROWS // 128, 128), centroids)
    return (*adam_update(centroids, first_moment, second_moment, gradient), loss[0, 0])


def solution(mesh):
    split = Mesh(mesh.devices.reshape(NX, NZ, NY, NC), AXES)
    placed = (P(DP, None), P(), P(DP_MP, None), P(DP_MP, None), P(DP_MP, None))
    return jax.shard_map(
        shards,
        mesh=split,
        in_specs=placed,
        out_specs=(P(DP_MP, None), P(DP_MP, None), P(DP_MP, None), P()),
        check_vma=False,
    )
```

time: 220 us -> 70.7 us (0.32)
  waiting for transfers between devices: 125 us -> 0 us
  Pallas kernels: 0 us -> 64.1 us
  blocking collectives: 56.6 us -> 0 us
  matrix products: 17.9 us -> 0 us
  between operations: 16 us -> 2.49 us
  other arithmetic: 4.04 us -> 1.14 us
  local copies, waits for them, and re-layouts: 0.03 us -> 2.75 us
    all_gather x1 -> x0, waiting for transfers between devices: 124 us -> none  [shards(): gathered = lax.all_gather(query_emb, DP, axis=0, tiled=True)]
    pallas_call x0 -> x1, Pallas kernels: none -> 64.1 us  [shards(): pl.pallas_call(kernel, name='step', out_shape=(jax.ShapeDtypeStruct((OWN,...]
    all_gather x4 -> x0, blocking collectives: 56.6 us -> none  [all_in_one(): both, at, found = (lax.all_gather(jnp.concatenate(lines), axis), 0, {})]
    dot_general x2 -> x0, matrix products: 17.9 us -> none  [the longest x1 9.24 us: shards(): jnp.einsum('rk,rd->kd', weights, gathered, preferred_element_type=jnp.flo...]
    unnamed x10, local copies, waits for them, and re-layouts: 0.03 us -> 2.75 us
  transfers between devices with their start and end apart: 1 -> 0, of which waited for: 1 -> 0; matrix products, arithmetic and copies ran while one was open for 0% -> 0% of each run, Pallas kernels for 0% -> 0%
where the time goes in v1:
time: 70.7 us; the launch traced here: 70.5 us
  Pallas kernels  64.1 us (91%)
  local copies, waits for them, and re-layouts  2.75 us (4%)
  between operations  2.49 us (4%)
  other arithmetic  1.14 us (2%)
    pallas_call x1, Pallas kernels, shards(): pl.pallas_call(kernel, name='step', out_shape=(jax.ShapeDtypeStruct((OWN,...  64.1 us
    unnamed x10, local copies, waits for them, and re-layouts  2.75 us

profile of v1, /device:TPU:1, one launch (start us, length us, event | category | flops | bytes accessed | tf_op | source)
XLA Modules:
  0.0 70.5 jit_solution(3293620537238091144)
XLA Ops:
  0.6 0.0 copy-start
  0.6 1.0 %copy-done = f32[128,768]{1,0:T(8,128)S(1)} copy-done((f32[128,768]{1,0:T(8,128)S(1)}, f32[128,768]{1,0:T(8,128)}, u32[]{:S(2)}) %copy-start) | copy-done | bytes 393240
  1.6 0.0 copy-start.1
  1.6 1.0 %copy-done.1 = bf16[256,768]{1,0:T(8,128)(2,1)S(1)} copy-done((bf16[256,768]{1,0:T(8,128)(2,1)S(1)}, bf16[256,768]{1,0:T(8,128)(2,1)}, u32[]{:S(2)}) %copy-start.1) | copy-done | bytes 393240
  2.6 0.0 copy-start.2
  2.6 0.8 %copy-done.2 = s32[8192]{0:T(1024)S(1)} copy-done((s32[8192]{0:T(1024)S(1)}, s32[8192]{0:T(1024)}, u32[]{:S(2)}) %copy-start.2) | copy-done | bytes 32792
  3.4 0.0 copy-start.3
  3.4 0.0 copy-start.4
  3.4 64.1 %step.1 = (f32[128,768]{1,0:T(8,128)S(1)}, f32[1,1]{1,0:T(1,128)}) custom-call(bf16[256,768]{1,0:T(8,128)(2,1)S(1)} %copy-done.1, s32[64,128]{1,0:T(8,128)S(1)} %bitcast.2, f32[128,768]{1,0:T(8,128)S(1)} %copy-done), custom_call_target="tpu_custom_call" | custom-call | tf_op jit(solution)/shard_map/step/pallas_call | solution.py:355
  67.5 0.0 copy-done.3
  67.5 0.0 copy-done.4
  67.5 1.1 %divide_subtract_fusion = (f32[128,768]{1,0:T(8,128)}, f32[128,768]{1,0:T(8,128)}, f32[128,768]{1,0:T(8,128)}) fusion(f32[128,768]{1,0:T(8,128)S(1)} %copy-done, f32[128,768]{1,0:T(8,128)S(1)} %get-tuple-element.6, f32[128,768]{1,0:T(8,128)S(1)} %copy-done.3, f32[128,768]{1,0:T(8,128)S(1)} %copy-done.4), kind=kLoop, calls=%fused_computation.2 | loop fusion | flops 1081344 | bytes 2752512 | tf_op jit(solution)/shard_map/sub | solution.py:38
Async XLA Ops:
  0.6 1.0 %copy-start = (f32[128,768]{1,0:T(8,128)S(1)}, f32[128,768]{1,0:T(8,128)}, u32[]{:S(2)}) copy-start(f32[128,768]{1,0:T(8,128)} %cent_ref.1) | copy-start | bytes 1179652
  1.6 1.0 %copy-start.1 = (bf16[256,768]{1,0:T(8,128)(2,1)S(1)}, bf16[256,768]{1,0:T(8,128)(2,1)}, u32[]{:S(2)}) copy-start(bf16[256,768]{1,0:T(8,128)(2,1)} %query_hbm.1) | copy-start | bytes 1179652
  2.6 0.8 %copy-start.2 = (s32[8192]{0:T(1024)S(1)}, s32[8192]{0:T(1024)}, u32[]{:S(2)}) copy-start(s32[8192]{0:T(1024)} %param.6) | copy-start | bytes 98308
  3.4 64.1 %copy-start.3 = (f32[128,768]{1,0:T(8,128)S(1)}, f32[128,768]{1,0:T(8,128)}, u32[]{:S(2)}) copy-start(f32[128,768]{1,0:T(8,128)} %param.8) | copy-start | bytes 1179652
  3.4 64.1 %copy-start.4 = (f32[128,768]{1,0:T(8,128)S(1)}, f32[128,768]{1,0:T(8,128)}, u32[]{:S(2)}) copy-start(f32[128,768]{1,0:T(8,128)} %param.9) | copy-start | bytes 1179652

commit v2 on v0

v2 whole, which is shorter than its diff:
```python
import jax
import jax.numpy as jnp
from jax import lax
from jax.experimental import pallas as pl
from jax.experimental.pallas import tpu as pltpu
from jax.sharding import Mesh
from jax.sharding import PartitionSpec as P

NX, NZ, NY, NC = 4, 8, 4, 2
AXES = ("x", "z", "y", "c")
DP = ("x", "z")
DP_MP = ("x", "z", "y", "c")
MESH = pl.DeviceIdType.MESH

ROWS = 8192
D = 768
LISTS = 32768
BLOCKS = NX * NZ
CLASSES = 4
BLOCK_ROWS = ROWS // BLOCKS // CLASSES
DEV_ROWS = BLOCKS * BLOCK_ROWS
OWN = LISTS // (NX * NZ * NY * NC)
HELD = 4 * OWN
TILES = DEV_ROWS // 128
GROUP = 4 * BLOCK_ROWS
PIECES = 2
PIECE = BLOCK_ROWS // PIECES
SENDS = 31 * PIECES
PARTS = 6
WIDTH = D // PARTS

beta_first = 0.9
beta_second = 0.95
learn_rate = 0.01
epsilon = 1e-08


def adam_update(centroids, first_moment, second_moment, gradient):
    new_first = beta_first * first_moment + (1.0 - beta_first) * gradient
    new_second = beta_second * second_moment + (1.0 - beta_second) * gradient * gradient
    new_centroids = centroids - learn_rate * new_first / (jnp.sqrt(new_second) + epsilon)
    return (new_centroids, new_first, new_second)


def log_sum_exp(slots):
    top = slots[0]
    for part in slots[1:]:
        top = jnp.maximum(top, part)
    total = jnp.exp(slots[0] - top)
    for part in slots[1:]:
        total = total + jnp.exp(part - top)
    return top + jnp.log(total)


STARTS = [('UDLR', 'dRuDLUr'), ('UDRL', 'UdDLR')]
CUTS = ((17, 41, 45, 55, 59, 62, 62, 62), (21, 32, 44, 56, 60, 62, 62, 62))
GROUPS = ((0, 1, -1, -2, 2, -3, 3, 4), (0, 1, -1, -2, 2, -3, 3, 4))
ROUTES = (
    (
        (-1, 0, 0, ""), (1, 0, 0, "L"), (0, -1, 0, "URL"), (0, 1, 0, "DLR"), (-1, 0, 1, "UD"), (1, 0, 1, "U"),
        (0, -2, 1, "U"), (0, -1, 1, ""), (0, 2, 1, "LRD"), (0, 1, 1, "L"), (2, 0, 1, ""), (2, 0, 0, "U"),
        (-1, -1, 0, ""), (0, -2, 0, "rRLU"), (1, -1, 0, ""), (0, 2, 0, "DR"), (-1, 1, 0, ""), (-1, -1, 1, "RU"),
        (1, 1, 0, "DL"), (-1, 1, 1, ""), (1, -1, 1, "U"), (1, 2, 1, "D"), (-1, 2, 1, "D"), (0, 3, 1, ""),
        (0, -3, 1, "LRU"), (1, 1, 1, "L"), (2, -1, 0, ""), (0, 3, 0, "DLR"), (1, -2, 0, "U"), (0, -3, 0, ""),
        (1, 2, 0, "L"), (2, -2, 0, "U"), (2, 1, 0, ""), (-1, -2, 0, "U"), (-1, -2, 1, ""), (1, 3, 1, "DL"),
        (1, -3, 1, "L"), (-1, 2, 0, ""), (1, -2, 1, ""), (-1, 3, 1, "D"), (2, 1, 1, "D"), (2, -1, 1, "U"),
        (0, 4, 1, ""), (0, 4, 0, "R"), (1, 3, 0, "DL"), (1, -3, 0, ""), (-1, -3, 1, ""), (2, -3, 0, "U"),
        (2, 2, 0, ""), (1, 4, 1, "L"), (-1, -3, 0, ""), (-1, 3, 0, ""), (2, 3, 1, ""), (-1, 4, 1, ""),
        (2, -2, 1, ""), (2, 2, 1, ""), (2, -3, 1, ""), (-1, 4, 0, ""), (1, 4, 0, ""), (2, 3, 0, ""), (2, 4, 0, ""),
        (2, 4, 1, ""),
    ),
    (
        (-1, 0, 0, "R"), (1, 0, 0, ""), (0, -1, 0, "ULR"), (0, 1, 0, "DLR"), (-1, 0, 1, "R"), (1, 0, 1, "DU"),
        (0, -1, 1, "UR"), (1, -1, 0, "L"), (0, 2, 1, "D"), (2, 0, 0, "D"), (0, -2, 0, "LUR"), (0, 1, 1, "R"),
        (1, 1, 0, "D"), (-1, -1, 0, ""), (1, -1, 1, ""), (0, 2, 0, "DR"), (-1, 1, 0, ""), (0, -2, 1, "UL"),
        (2, -1, 0, ""), (1, 1, 1, "DL"), (2, 0, 1, ""), (0, -3, 0, "R"), (1, -2, 0, "UL"), (0, 3, 1, "L"),
        (-1, -1, 1, "RU"), (2, 1, 0, ""), (1, -2, 1, "U"), (0, -3, 1, "RU"), (-1, -2, 0, ""), (1, 2, 0, ""),
        (2, 1, 1, ""), (-1, 1, 1, "D"), (1, -3, 0, "L"), (0, 3, 0, "RDL"), (2, -2, 0, ""), (-1, 2, 0, "R"),
        (-1, -2, 1, ""), (1, 2, 1, ""), (1, 3, 1, "LD"), (-1, -3, 0, ""), (1, -3, 1, ""), (-1, 2, 1, "DR"),
        (2, -3, 0, "U"), (2, -1, 1, "U"), (0, 4, 1, ""), (0, 4, 0, "L"), (1, 3, 0, ""), (-1, -3, 1, "UR"),
        (1, 4, 1, ""), (-1, 3, 0, "DR"), (2, 3, 1, "D"), (2, 4, 0, ""), (2, 2, 0, ""), (-1, 3, 1, ""), (1, 4, 0, ""),
        (2, -2, 1, ""), (2, 2, 1, ""), (2, -3, 1, ""), (-1, 4, 1, ""), (-1, 4, 0, ""), (2, 3, 0, ""), (2, 4, 1, ""),
    ),
)


def kernel(
    query_hbm, pos_hbm, cent_hbm, grad_ref, loss_ref,
    q, pos, cent, chosen, table, logits, weights, norm, hit, stat1, stat2, hit1, loss2, loss,
    part, from_partner, y_out, y_in,
    own_sem, q_send, q_recv, t_send, t_recv,
    s1_send, s1_recv, s2_send, s2_recv, h1_send, h1_recv, h2_send, h2_recv, l_send, l_recv,
    d_send, d_recv, y_send, y_recv,
):
    x, z, y, c = (lax.axis_index(a) for a in AXES)
    turn = 1 - 2 * c

    def at_x(k):
        return lax.rem(x + (k + NX), NX)

    def at_z(k):
        return lax.rem(z + (k + NZ), NZ)

    def at_y(k):
        return lax.rem(y + (k + NY), NY)

    helper_y = at_y(turn)
    owner_y = at_y(-turn)
    other = 1 - c
    partner = {"c": other}

    group1 = [(dx, dy) for dy in (0, 2) for dx in range(NX) if (dx, dy) != (0, 0)]
    peers = [{"x": at_x(dx)} for dx in (1, -1, 2)]
    peers += [{"z": at_z(dz)} for dz in (1, -1, 2, -2)]
    peers += [{"y": at_y(1)}, {"y": at_y(-1)}, partner, {"y": helper_y, "c": other}]
    barrier = pltpu.get_barrier_semaphore()
    for peer in peers:
        pl.semaphore_signal(barrier, inc=1, device_id=peer, device_id_type=MESH)

    def remote(src, dst, send, recv, where):
        copy = pltpu.make_async_remote_copy(
            src_ref=src, dst_ref=dst, send_sem=send, recv_sem=recv, device_id=where, device_id_type=MESH
        )
        copy.start()
        return copy

    def arrived(dst, sem):
        pltpu.make_async_copy(dst, dst, sem).wait()

    row_class = lax.rem(y, 2) * 2 + c
    own_place = z * NX + x
    local = [
        pltpu.make_async_copy(
            query_hbm.at[pl.ds(pl.multiple_of(row_class * BLOCK_ROWS + p * PIECE, PIECE), PIECE)],
            q.at[own_place, p],
            own_sem.at[p],
        )
        for p in range(PIECES)
    ]
    local.append(pltpu.make_async_copy(cent_hbm, cent, own_sem.at[PIECES]))
    local.append(pltpu.make_async_copy(pos_hbm, pos, own_sem.at[PIECES + 1]))
    for copy in local:
        copy.start()
    for copy in local:
        copy.wait()
    table[0] = cent[...].astype(jnp.bfloat16)
    pl.semaphore_wait(barrier, len(peers))

    toward = {"R": {"x": at_x(1)}, "L": {"x": at_x(-1)}, "U": {"z": at_z(1)}, "D": {"z": at_z(-1)}}
    toward |= {"r": {"x": at_x(2)}, "l": {"x": at_x(2)}, "u": {"z": at_z(2)}, "d": {"z": at_z(-2)}}

    def carrier():
        count = [0]

        def send(dx, dz, p, links):
            place = at_z(dz) * NX + at_x(dx)
            for link in links:
                remote(
                    q.at[place, p], q.at[place, p], q_send.at[count[0]], q_recv.at[place * PIECES + p], toward[link]
                )
                count[0] += 1

        return send, count

    carriers = [carrier() for _ in range(NC)]

    def move(r):
        for core in range(NC):
            send, _ = carriers[core]
            cuts = (0, *CUTS[core])
            events = ROUTES[core][cuts[r] : cuts[r + 1]]

            @pl.when(c == core)
            def _(send=send, core=core, events=events):
                if r == 0:
                    for p in range(PIECES):
                        send(0, 0, p, STARTS[core][p])
                for dx, dz, p, links in events:
                    place = at_z(dz) * NX + at_x(dx)
                    arrived(q.at[place, p], q_recv.at[place * PIECES + p])
                    send(dx, dz, p, links)

    parity = lax.rem(y, 2)
    lane = lax.broadcasted_iota(jnp.int32, (1, 128), 1)

    def targets(bz, bx):
        return pos[pl.ds((bx * NZ + bz) * 2 + parity, 1), :]

    def choose():
        for j in range(TILES):
            r0, r1 = targets(j // 2, 2 * (j % 2)), targets(j // 2, 2 * (j % 2) + 1)
            low = jnp.where(c == 0, r0, pltpu.roll(r0, 64, 1))
            high = jnp.where(c == 0, pltpu.roll(r1, 64, 1), r1)
            chosen[j : j + 1, :] = jnp.where(lane < 64, low, high)

    sub = lax.broadcasted_iota(jnp.int32, (OWN, 128), 0)
    first_block = (x * NZ + z) * NY * NC
    held = [(y, c), (y, other), (owner_y, c), (helper_y, other)]
    firsts = [(first_block + hy * NC + hc) * OWN for hy, hc in held]

    def group_logits(r):
        group = jnp.where(c == 0, at_z(GROUPS[0][r]), at_z(GROUPS[1][r]))
        start = pl.multiple_of(group * GROUP, GROUP)
        rows = q[pl.ds(group * NX, NX)].reshape(GROUP, D)
        block = lax.dot_general(
            table[...].reshape(HELD, D), rows, (((1,), (1,)), ((), ())), preferred_element_type=jnp.float32
        )
        logits[:, pl.ds(start, GROUP)] = block
        peak = jnp.max(block, axis=0, keepdims=True)
        mass = jnp.sum(jnp.exp(block - peak), axis=0, keepdims=True)
        local_norm = peak + jnp.log(mass)
        for h in range(2):
            tile = group * 2 + h
            norm[pl.ds(tile, 1), :] = local_norm[:, h * 128 : h * 128 + 128]
            ids = chosen[pl.ds(tile, 1), :]
            found = jnp.zeros((1, 128), jnp.float32)
            for k in range(4):
                values = block[k * OWN : (k + 1) * OWN, h * 128 : h * 128 + 128]
                found = found + jnp.sum(jnp.where(sub + firsts[k] == ids, values, 0.0), axis=0, keepdims=True)
            hit[pl.ds(tile, 1), :] = found

    table_sends = [
        remote(table.at[0], table.at[1], t_send.at[0], t_recv.at[0], partner),
        remote(table.at[0], table.at[2], t_send.at[1], t_recv.at[1], {"y": helper_y}),
        remote(table.at[0], table.at[3], t_send.at[2], t_recv.at[2], {"y": helper_y, "c": other}),
    ]
    for r in range(8):
        move(r)
        if r == 0:
            choose()
            for k in range(3):
                arrived(table.at[k + 1], t_recv.at[k])
        group_logits(r)
    for _, count in carriers:
        assert count[0] == SENDS

    me1 = lax.div(y, 2) * NX + x

    def exchange1(slots, send, recv):
        for k, (dx, dy) in enumerate(group1):
            remote(slots.at[me1], slots.at[me1], send.at[k], recv.at[me1], {"x": at_x(dx), "y": at_y(dy)})

    def wait1(slots, send, recv):
        for k, (dx, dy) in enumerate(group1):
            place = lax.div(at_y(dy), 2) * NX + at_x(dx)
            arrived(slots.at[place], recv.at[place])
            arrived(slots.at[0], send.at[k])

    def exchange2(slots, send, recv):
        for dz in range(1, NZ):
            remote(slots.at[z], slots.at[z], send.at[dz - 1], recv.at[z], {"z": at_z(dz)})

    def wait2(slots, send, recv):
        for dz in range(1, NZ):
            arrived(slots.at[at_z(dz)], recv.at[at_z(dz)])
            arrived(slots.at[0], send.at[dz - 1])

    def summed(slots):
        total = slots[0]
        for k in range(1, 8):
            total = total + slots[k]
        return total

    stat1[me1] = norm[...]
    exchange1(stat1, s1_send, s1_recv)
    hit1[me1] = hit[...]
    exchange1(hit1, h1_send, h1_recv)
    wait1(stat1, s1_send, s1_recv)
    stat2[z] = log_sum_exp([stat1[k] for k in range(8)])
    exchange2(stat2, s2_send, s2_recv)
    wait2(stat2, s2_send, s2_recv)
    norm[...] = log_sum_exp([stat2[k] for k in range(8)])

    wait1(hit1, h1_send, h1_recv)
    here = lax.rem(lax.div(chosen[...], OWN * NY * NC), NZ) == z
    missed = jnp.where(here, norm[...] - summed(hit1), 0.0)
    loss2[z] = missed[:8] + missed[8:]
    exchange2(loss2, h2_send, h2_recv)

    def tile_weights(j, carry):
        start = pl.multiple_of(j * 128, 128)
        log_norm = norm[pl.ds(j, 1), :]
        ids = chosen[pl.ds(j, 1), :]
        for k in (2, 3, 0, 1):
            soft = jnp.exp(logits[pl.ds(k * OWN, OWN), pl.ds(start, 128)] - log_norm)
            soft = jnp.where(sub + firsts[k] == ids, soft - 1.0, soft)
            weights[pl.ds(k * OWN, OWN), pl.ds(start, 128)] = soft.astype(jnp.bfloat16)
        return carry

    lax.fori_loop(0, TILES, tile_weights, 0)

    def pair_gradient(first, n):
        part[n, first * OWN : (first + 2) * OWN, :] = jnp.dot(
            weights[first * OWN : (first + 2) * OWN, :],
            q[:, :, :, n * WIDTH : (n + 1) * WIDTH].reshape(DEV_ROWS, WIDTH),
            preferred_element_type=jnp.float32,
        )

    to_partner, to_owner = [], []

    def hand_over(n, slot):
        lists = part.at[n, pl.ds((1 + 2 * slot) * OWN, OWN)]
        to_partner.append(remote(lists, from_partner.at[n, slot], d_send.at[n, slot], d_recv.at[n, slot], partner))

    def give_back(n):
        arrived(from_partner.at[n, 1], d_recv.at[n, 1])
        y_out[n] = part[n, 2 * OWN : 3 * OWN, :] + from_partner[n, 1]
        to_owner.append(remote(y_out.at[n], y_in.at[n], y_send.at[n], y_recv.at[n], {"y": owner_y}))

    for n in range(PARTS):
        pair_gradient(2, n)
        hand_over(n, 1)
        if n:
            give_back(n - 1)
    give_back(PARTS - 1)
    wait2(loss2, h2_send, h2_recv)
    loss[0] = summed(loss2)
    loss_across = remote(loss.at[0], loss.at[1], l_send.at[0], l_recv.at[0], partner)
    for n in range(PARTS):
        pair_gradient(0, n)
        hand_over(n, 0)
    loss_across.wait()
    loss[2] = loss[0] + loss[1]
    loss_back = remote(loss.at[2], loss.at[3], l_send.at[1], l_recv.at[1], {"y": owner_y})
    for n in range(PARTS):
        arrived(from_partner.at[n, 0], d_recv.at[n, 0])
        arrived(y_in.at[n], y_recv.at[n])
        grad_ref[:, n * WIDTH : (n + 1) * WIDTH] = part[n, :OWN, :] + from_partner[n, 0] + y_in[n]
    loss_back.wait()
    loss_ref[...] = jnp.sum(loss[2] + loss[3], keepdims=True) * (1.0 / ROWS)

    for k in range(SENDS):
        arrived(q.at[0, 0], q_send.at[k])
    for copy in table_sends + to_partner + to_owner:
        copy.wait_send()


def shards(query_emb, positive_list, centroids, first_moment, second_moment):
    f32, bf16, i32, dma = jnp.float32, jnp.bfloat16, jnp.int32, pltpu.SemaphoreType.DMA
    vmem, hbm = pl.BlockSpec(memory_space=pltpu.VMEM), pl.BlockSpec(memory_space=pl.ANY)
    gradient, loss = pl.pallas_call(
        kernel,
        name="step",
        out_shape=(jax.ShapeDtypeStruct((OWN, D), f32), jax.ShapeDtypeStruct((1, 1), f32)),
        in_specs=[hbm, hbm, hbm],
        out_specs=(vmem, vmem),
        scratch_shapes=[
            pltpu.VMEM((BLOCKS, PIECES, PIECE, D), bf16),
            pltpu.VMEM((ROWS // 128, 128), i32),
            pltpu.VMEM((OWN, D), f32),
            pltpu.VMEM((TILES, 128), i32),
            pltpu.VMEM((4, OWN, D), bf16),
            pltpu.VMEM((HELD, DEV_ROWS), f32),
            pltpu.VMEM((HELD, DEV_ROWS), bf16),
            pltpu.VMEM((TILES, 128), f32),
            pltpu.VMEM((TILES, 128), f32),
            pltpu.VMEM((8, TILES, 128), f32),
            pltpu.VMEM((8, TILES, 128), f32),
            pltpu.VMEM((8, TILES, 128), f32),
            pltpu.VMEM((8, 8, 128), f32),
            pltpu.VMEM((4, 8, 128), f32),
            pltpu.VMEM((PARTS, HELD, WIDTH), f32),
            pltpu.VMEM((PARTS, 2, OWN, WIDTH), f32),
            pltpu.VMEM((PARTS, OWN, WIDTH), f32),
            pltpu.VMEM((PARTS, OWN, WIDTH), f32),
            dma((PIECES + 2,)), dma((SENDS,)), dma((BLOCKS * PIECES,)), dma((3,)), dma((3,)),
            dma((7,)), dma((8,)), dma((7,)), dma((8,)), dma((7,)), dma((8,)), dma((7,)), dma((8,)), dma((2,)), dma((2,)),
            dma((PARTS, 2)), dma((PARTS, 2)), dma((PARTS,)), dma((PARTS,)),
        ],
        compiler_params=pltpu.CompilerParams(collective_id=0, has_side_effects=True, vmem_limit_bytes=56000000),
    )(query_emb, positive_list.reshape(ROWS // 128, 128), centroids)
    return (*adam_update(centroids, first_moment, second_moment, gradient), loss[0, 0])


def solution(mesh):
    split = Mesh(mesh.devices.reshape(NX, NZ, NY, NC), AXES)
    placed = (P(DP, None), P(), P(DP_MP, None), P(DP_MP, None), P(DP_MP, None))
    return jax.shard_map(
        shards,
        mesh=split,
        in_specs=placed,
        out_specs=(P(DP_MP, None), P(DP_MP, None), P(DP_MP, None), P()),
        check_vma=False,
    )
```

time: 220 us -> 62 us (0.28)
  waiting for transfers between devices: 125 us -> 0 us
  blocking collectives: 56.6 us -> 0 us
  Pallas kernels: 0 us -> 56.5 us
  matrix products: 17.9 us -> 0 us
  between operations: 16 us -> 2.41 us
    all_gather x1 -> x0, waiting for transfers between devices: 124 us -> none  [shards(): gathered = lax.all_gather(query_emb, DP, axis=0, tiled=True)]
    all_gather x4 -> x0, blocking collectives: 56.6 us -> none  [all_in_one(): both, at, found = (lax.all_gather(jnp.concatenate(lines), axis), 0, {})]
    pallas_call x0 -> x1, Pallas kernels: none -> 56.5 us  [shards(): pl.pallas_call(kernel, name='step', out_shape=(jax.ShapeDtypeStruct((OWN,...]
    dot_general x2 -> x0, matrix products: 17.9 us -> none  [the longest x1 9.24 us: shards(): jnp.einsum('rk,rd->kd', weights, gathered, preferred_element_type=jnp.flo...]
  transfers between devices with their start and end apart: 1 -> 0, of which waited for: 1 -> 0; matrix products, arithmetic and copies ran while one was open for 0% -> 0% of each run, Pallas kernels for 0% -> 0%
where the time goes in v2:
time: 62 us; the launch traced here: 61.8 us
  Pallas kernels  56.5 us (91%)
  between operations  2.41 us (4%)
  other arithmetic  2.13 us (3%)
  local copies, waits for them, and re-layouts  0.76 us (1%)
    pallas_call x1, Pallas kernels, shards(): pl.pallas_call(kernel, name='step', out_shape=(jax.ShapeDtypeStruct((OWN,...  56.5 us
    sub x1, other arithmetic, adam_update(): centroids - learn_rate * new_first / (jnp.sqrt(new_second) + epsilon)  2.13 us

profile of v2, /device:TPU:1, one launch (start us, length us, event | category | flops | bytes accessed | tf_op | source)
XLA Modules:
  0.0 61.8 jit_solution(1497157849008107332)
XLA Ops:
  0.6 0.0 copy-start
  0.6 0.7 %copy-done = s32[8192]{0:T(1024)S(1)} copy-done((s32[8192]{0:T(1024)S(1)}, s32[8192]{0:T(1024)}, u32[]{:S(2)}) %copy-start) | copy-done | bytes 32792
  1.4 0.0 copy-start.1
  1.4 0.0 copy-start.2
  1.4 56.5 %step.1 = (f32[128,768]{1,0:T(8,128)S(1)}, f32[1,1]{1,0:T(1,128)}) custom-call(bf16[256,768]{1,0:T(8,128)(2,1)} %query_hbm.1, s32[64,128]{1,0:T(8,128)S(1)} %bitcast.2, f32[128,768]{1,0:T(8,128)} %cent_hbm.1), custom_call_target="tpu_custom_call" | custom-call | tf_op jit(solution)/shard_map/step/pallas_call | solution.py:341
  57.9 0.0 copy-done.1
  57.9 0.0 copy-done.2
  57.9 2.1 %divide_subtract_fusion = (f32[128,768]{1,0:T(8,128)}, f32[128,768]{1,0:T(8,128)}, f32[128,768]{1,0:T(8,128)}) fusion(f32[128,768]{1,0:T(8,128)S(1)} %copy-done.1, f32[128,768]{1,0:T(8,128)S(1)} %get-tuple-element.6, f32[128,768]{1,0:T(8,128)S(1)} %copy-done.2, f32[128,768]{1,0:T(8,128)} %param.9), kind=kLoop, calls=%fused_computation.2 | loop fusion | flops 1081344 | bytes 2752512 | tf_op jit(solution)/shard_map/sub | solution.py:41
Async XLA Ops:
  0.6 0.8 %copy-start = (s32[8192]{0:T(1024)S(1)}, s32[8192]{0:T(1024)}, u32[]{:S(2)}) copy-start(s32[8192]{0:T(1024)} %param.6) | copy-start | bytes 98308
  1.4 56.5 %copy-start.1 = (f32[128,768]{1,0:T(8,128)S(1)}, f32[128,768]{1,0:T(8,128)}, u32[]{:S(2)}) copy-start(f32[128,768]{1,0:T(8,128)} %cent_hbm.1) | copy-start | bytes 1179652
  1.4 56.5 %copy-start.2 = (f32[128,768]{1,0:T(8,128)S(1)}, f32[128,768]{1,0:T(8,128)}, u32[]{:S(2)}) copy-start(f32[128,768]{1,0:T(8,128)} %param.8) | copy-start | bytes 1179652

commit v3 on v2

--- a/solution.py
+++ b/solution.py
@@ -26,7 +26,8 @@
 PIECES = 2
 PIECE = BLOCK_ROWS // PIECES
 SENDS = 31 * PIECES
-PARTS = 6
+HALF = OWN // 2
+PARTS = 3
 WIDTH = D // PARTS
 
 beta_first = 0.9
@@ -52,34 +53,34 @@
     return top + jnp.log(total)
 
 
-STARTS = [('UDLR', 'dRuDLUr'), ('UDRL', 'UdDLR')]
-CUTS = ((17, 41, 45, 55, 59, 62, 62, 62), (21, 32, 44, 56, 60, 62, 62, 62))
-GROUPS = ((0, 1, -1, -2, 2, -3, 3, 4), (0, 1, -1, -2, 2, -3, 3, 4))
+STARTS = [('DURL', 'udLrRDU'), ('URDL', 'UDLR')]
+CUTS = ((16, 33, 41, 46, 51, 57, 61, 62), (20, 35, 39, 43, 47, 57, 61, 62))
+GROUPS = ((0, 1, -1, 2, -2, -3, 3, 4), (0, 1, -2, -1, 2, -3, 3, 4))
 ROUTES = (
     (
-        (-1, 0, 0, ""), (1, 0, 0, "L"), (0, -1, 0, "URL"), (0, 1, 0, "DLR"), (-1, 0, 1, "UD"), (1, 0, 1, "U"),
-        (0, -2, 1, "U"), (0, -1, 1, ""), (0, 2, 1, "LRD"), (0, 1, 1, "L"), (2, 0, 1, ""), (2, 0, 0, "U"),
-        (-1, -1, 0, ""), (0, -2, 0, "rRLU"), (1, -1, 0, ""), (0, 2, 0, "DR"), (-1, 1, 0, ""), (-1, -1, 1, "RU"),
-        (1, 1, 0, "DL"), (-1, 1, 1, ""), (1, -1, 1, "U"), (1, 2, 1, "D"), (-1, 2, 1, "D"), (0, 3, 1, ""),
-        (0, -3, 1, "LRU"), (1, 1, 1, "L"), (2, -1, 0, ""), (0, 3, 0, "DLR"), (1, -2, 0, "U"), (0, -3, 0, ""),
-        (1, 2, 0, "L"), (2, -2, 0, "U"), (2, 1, 0, ""), (-1, -2, 0, "U"), (-1, -2, 1, ""), (1, 3, 1, "DL"),
-        (1, -3, 1, "L"), (-1, 2, 0, ""), (1, -2, 1, ""), (-1, 3, 1, "D"), (2, 1, 1, "D"), (2, -1, 1, "U"),
-        (0, 4, 1, ""), (0, 4, 0, "R"), (1, 3, 0, "DL"), (1, -3, 0, ""), (-1, -3, 1, ""), (2, -3, 0, "U"),
-        (2, 2, 0, ""), (1, 4, 1, "L"), (-1, -3, 0, ""), (-1, 3, 0, ""), (2, 3, 1, ""), (-1, 4, 1, ""),
-        (2, -2, 1, ""), (2, 2, 1, ""), (2, -3, 1, ""), (-1, 4, 0, ""), (1, 4, 0, ""), (2, 3, 0, ""), (2, 4, 0, ""),
-        (2, 4, 1, ""),
+        (-1, 0, 0, "R"), (1, 0, 0, ""), (0, -1, 0, "uURL"), (0, 1, 0, "DRL"), (1, 0, 1, "U"), (2, 0, 1, "D"),
+        (0, -2, 1, "UrR"), (0, 2, 1, "LRD"), (-1, 0, 1, "UD"), (0, -1, 1, ""), (0, 1, 1, "L"), (2, 0, 0, "D"),
+        (1, -1, 0, ""), (0, 2, 0, "LDR"), (-1, -1, 0, "R"), (1, 1, 0, ""), (0, -3, 0, "RUL"), (-1, 1, 0, ""),
+        (0, -2, 0, "LR"), (1, 2, 1, "D"), (2, 1, 1, "D"), (1, -1, 1, "UL"), (1, 1, 1, ""), (0, 3, 1, ""),
+        (0, -3, 1, "UR"), (2, -2, 1, "U"), (-1, -2, 1, ""), (1, 2, 0, "L"), (-1, 1, 1, ""), (-1, -1, 1, ""),
+        (-1, 2, 1, "D"), (1, -3, 0, "U"), (2, 1, 0, ""), (0, 4, 0, "r"), (-1, 2, 0, ""), (2, -1, 0, ""),
+        (1, -2, 0, "L"), (0, 3, 0, "RL"), (1, -2, 1, "U"), (-1, -3, 0, "UR"), (2, -1, 1, ""), (1, 3, 1, "DL"),
+        (0, 4, 1, "R"), (-1, -2, 0, ""), (2, 2, 0, "D"), (2, 2, 1, ""), (2, -3, 1, "U"), (-1, -3, 1, ""),
+        (-1, 3, 1, ""), (1, 4, 0, ""), (2, -2, 0, ""), (1, -3, 1, ""), (2, 4, 0, ""), (-1, 3, 0, ""), (1, 3, 0, ""),
+        (1, 4, 1, ""), (2, -3, 0, ""), (-1, 4, 0, ""), (2, 3, 1, ""), (2, 3, 0, ""), (-1, 4, 1, ""), (2, 4, 1, ""),
     ),
     (
-        (-1, 0, 0, "R"), (1, 0, 0, ""), (0, -1, 0, "ULR"), (0, 1, 0, "DLR"), (-1, 0, 1, "R"), (1, 0, 1, "DU"),
-        (0, -1, 1, "UR"), (1, -1, 0, "L"), (0, 2, 1, "D"), (2, 0, 0, "D"), (0, -2, 0, "LUR"), (0, 1, 1, "R"),
-        (1, 1, 0, "D"), (-1, -1, 0, ""), (1, -1, 1, ""), (0, 2, 0, "DR"), (-1, 1, 0, ""), (0, -2, 1, "UL"),
-        (2, -1, 0, ""), (1, 1, 1, "DL"), (2, 0, 1, ""), (0, -3, 0, "R"), (1, -2, 0, "UL"), (0, 3, 1, "L"),
-        (-1, -1, 1, "RU"), (2, 1, 0, ""), (1, -2, 1, "U"), (0, -3, 1, "RU"), (-1, -2, 0, ""), (1, 2, 0, ""),
-        (2, 1, 1, ""), (-1, 1, 1, "D"), (1, -3, 0, "L"), (0, 3, 0, "RDL"), (2, -2, 0, ""), (-1, 2, 0, "R"),
-        (-1, -2, 1, ""), (1, 2, 1, ""), (1, 3, 1, "LD"), (-1, -3, 0, ""), (1, -3, 1, ""), (-1, 2, 1, "DR"),
-        (2, -3, 0, "U"), (2, -1, 1, "U"), (0, 4, 1, ""), (0, 4, 0, "L"), (1, 3, 0, ""), (-1, -3, 1, "UR"),
-        (1, 4, 1, ""), (-1, 3, 0, "DR"), (2, 3, 1, "D"), (2, 4, 0, ""), (2, 2, 0, ""), (-1, 3, 1, ""), (1, 4, 0, ""),
-        (2, -2, 1, ""), (2, 2, 1, ""), (2, -3, 1, ""), (-1, 4, 1, ""), (-1, 4, 0, ""), (2, 3, 0, ""), (2, 4, 1, ""),
+        (-1, 0, 0, "D"), (1, 0, 0, "L"), (0, -1, 0, "URL"), (0, 1, 0, "DL"), (-1, 0, 1, "D"), (1, 0, 1, "DL"),
+        (0, -1, 1, "RUL"), (0, 1, 1, "D"), (2, 0, 0, "D"), (-1, -1, 0, "R"), (0, -2, 0, "UR"), (-1, 1, 0, "D"),
+        (1, -1, 0, "U"), (0, 2, 0, "LD"), (-1, -1, 1, "U"), (0, -2, 1, "UL"), (-1, 1, 1, ""), (1, 1, 0, ""),
+        (1, 1, 1, "DL"), (2, 0, 1, ""), (2, -1, 0, "U"), (0, -3, 0, "LU"), (0, 2, 1, "RD"), (1, -1, 1, "L"),
+        (-1, -2, 0, "U"), (1, -2, 0, ""), (2, 1, 0, ""), (1, 2, 0, "DL"), (-1, -2, 1, "RU"), (-1, 2, 0, "D"),
+        (1, -2, 1, ""), (0, -3, 1, "UL"), (-1, 2, 1, "DR"), (0, 3, 0, ""), (2, 1, 1, ""), (2, -2, 0, ""),
+        (1, 2, 1, "D"), (1, -3, 0, "L"), (2, -2, 1, "u"), (0, 4, 0, "RL"), (0, 3, 1, ""), (2, -1, 1, ""),
+        (-1, -3, 0, ""), (2, 2, 1, "D"), (1, 3, 0, ""), (2, 2, 0, ""), (-1, -3, 1, ""), (-1, 3, 0, "R"),
+        (1, -3, 1, "L"), (-1, 3, 1, "D"), (-1, 4, 0, ""), (0, 4, 1, "L"), (2, -3, 0, "U"), (1, 3, 1, ""),
+        (1, 4, 0, ""), (2, 3, 1, ""), (2, -3, 1, ""), (2, 3, 0, ""), (-1, 4, 1, ""), (2, 4, 1, ""), (1, 4, 1, ""),
+        (2, 4, 0, ""),
     ),
 )
 
@@ -93,7 +94,6 @@
     d_send, d_recv, y_send, y_recv,
 ):
     x, z, y, c = (lax.axis_index(a) for a in AXES)
-    turn = 1 - 2 * c
 
     def at_x(k):
         return lax.rem(x + (k + NX), NX)
@@ -104,15 +104,12 @@
     def at_y(k):
         return lax.rem(y + (k + NY), NY)
 
-    helper_y = at_y(turn)
-    owner_y = at_y(-turn)
     other = 1 - c
     partner = {"c": other}
 
     group1 = [(dx, dy) for dy in (0, 2) for dx in range(NX) if (dx, dy) != (0, 0)]
-    peers = [{"x": at_x(dx)} for dx in (1, -1, 2)]
-    peers += [{"z": at_z(dz)} for dz in (1, -1, 2, -2)]
-    peers += [{"y": at_y(1)}, {"y": at_y(-1)}, partner, {"y": helper_y, "c": other}]
+    peers = [{"x": at_x(k)} for k in (1, -1, 2)] + [{"z": at_z(k)} for k in (1, -1, 2, -2)]
+    peers += [partner] + [{"y": at_y(k), "c": core} for k in (1, -1) for core in (c, other)]
     barrier = pltpu.get_barrier_semaphore()
     for peer in peers:
         pl.semaphore_signal(barrier, inc=1, device_id=peer, device_id_type=MESH)
@@ -141,10 +138,9 @@
     local.append(pltpu.make_async_copy(pos_hbm, pos, own_sem.at[PIECES + 1]))
     for copy in local:
         copy.start()
-    for copy in local:
+    pl.semaphore_wait(barrier, len(peers))
+    for copy in local[:PIECES]:
         copy.wait()
-    table[0] = cent[...].astype(jnp.bfloat16)
-    pl.semaphore_wait(barrier, len(peers))
 
     toward = {"R": {"x": at_x(1)}, "L": {"x": at_x(-1)}, "U": {"z": at_z(1)}, "D": {"z": at_z(-1)}}
     toward |= {"r": {"x": at_x(2)}, "l": {"x": at_x(2)}, "u": {"z": at_z(2)}, "d": {"z": at_z(-2)}}
@@ -172,9 +168,6 @@
 
             @pl.when(c == core)
             def _(send=send, core=core, events=events):
-                if r == 0:
-                    for p in range(PIECES):
-                        send(0, 0, p, STARTS[core][p])
                 for dx, dz, p, links in events:
                     place = at_z(dz) * NX + at_x(dx)
                     arrived(q.at[place, p], q_recv.at[place * PIECES + p])
@@ -195,15 +188,17 @@
 
     sub = lax.broadcasted_iota(jnp.int32, (OWN, 128), 0)
     first_block = (x * NZ + z) * NY * NC
-    held = [(y, c), (y, other), (owner_y, c), (helper_y, other)]
-    firsts = [(first_block + hy * NC + hc) * OWN for hy, hc in held]
+    held = [(0, OWN, y, c, 0), (OWN, OWN, y, other, 0)]
+    for place, core in ((2 * OWN, c), (3 * OWN, other)):
+        held += [(place, HALF, at_y(-1), core, 0), (place + HALF, HALF, at_y(1), core, HALF)]
+    parts = [(place, lists, (first_block + hy * NC + hc) * OWN + first) for place, lists, hy, hc, first in held]
 
     def group_logits(r):
         group = jnp.where(c == 0, at_z(GROUPS[0][r]), at_z(GROUPS[1][r]))
         start = pl.multiple_of(group * GROUP, GROUP)
         rows = q[pl.ds(group * NX, NX)].reshape(GROUP, D)
         block = lax.dot_general(
-            table[...].reshape(HELD, D), rows, (((1,), (1,)), ((), ())), preferred_element_type=jnp.float32
+            table[...], rows, (((1,), (1,)), ((), ())), preferred_element_type=jnp.float32
         )
         logits[:, pl.ds(start, GROUP)] = block
         peak = jnp.max(block, axis=0, keepdims=True)
@@ -214,22 +209,43 @@
             norm[pl.ds(tile, 1), :] = local_norm[:, h * 128 : h * 128 + 128]
             ids = chosen[pl.ds(tile, 1), :]
             found = jnp.zeros((1, 128), jnp.float32)
-            for k in range(4):
-                values = block[k * OWN : (k + 1) * OWN, h * 128 : h * 128 + 128]
-                found = found + jnp.sum(jnp.where(sub + firsts[k] == ids, values, 0.0), axis=0, keepdims=True)
+            for place, lists, first in parts:
+                values = block[place : place + lists, h * 128 : h * 128 + 128]
+                found = found + jnp.sum(jnp.where(sub[:lists] == ids - first, values, 0.0), axis=0, keepdims=True)
             hit[pl.ds(tile, 1), :] = found
 
-    table_sends = [
-        remote(table.at[0], table.at[1], t_send.at[0], t_recv.at[0], partner),
-        remote(table.at[0], table.at[2], t_send.at[1], t_recv.at[1], {"y": helper_y}),
-        remote(table.at[0], table.at[3], t_send.at[2], t_recv.at[2], {"y": helper_y, "c": other}),
+    table_sends = []
+    table_routes = [
+        (0, 2 * OWN, HALF, {"y": at_y(1)}),
+        (1, 2 * OWN + HALF, HALF, {"y": at_y(-1)}),
+        (0, 3 * OWN, HALF, {"y": at_y(1), "c": other}),
+        (1, 3 * OWN + HALF, HALF, {"y": at_y(-1), "c": other}),
+        (0, OWN, OWN, partner),
     ]
+
+    def share_table():
+        local[PIECES].wait()
+        table[:OWN, :] = cent[...].astype(jnp.bfloat16)
+        for k, (half, place, rows, where) in enumerate(table_routes):
+            source, target = table.at[pl.ds(half * HALF, rows)], table.at[pl.ds(place, rows)]
+            table_sends.append(remote(source, target, t_send.at[k], t_recv.at[k], where))
+
+    for core in range(NC):
+        send, _ = carriers[core]
+
+        @pl.when(c == core)
+        def _(send=send, core=core):
+            for p in range(PIECES):
+                send(0, 0, p, STARTS[core][p])
+
+    share_table()
+    local[PIECES + 1].wait()
     for r in range(8):
         move(r)
         if r == 0:
             choose()
-            for k in range(3):
-                arrived(table.at[k + 1], t_recv.at[k])
+            for k, (_, place, rows, _) in enumerate(table_routes):
+                arrived(table.at[pl.ds(place, rows)], t_recv.at[k])
         group_logits(r)
     for _, count in carriers:
         assert count[0] == SENDS
@@ -277,17 +293,18 @@
     loss2[z] = missed[:8] + missed[8:]
     exchange2(loss2, h2_send, h2_recv)
 
-    def tile_weights(j, carry):
-        start = pl.multiple_of(j * 128, 128)
-        log_norm = norm[pl.ds(j, 1), :]
-        ids = chosen[pl.ds(j, 1), :]
-        for k in (2, 3, 0, 1):
-            soft = jnp.exp(logits[pl.ds(k * OWN, OWN), pl.ds(start, 128)] - log_norm)
-            soft = jnp.where(sub + firsts[k] == ids, soft - 1.0, soft)
-            weights[pl.ds(k * OWN, OWN), pl.ds(start, 128)] = soft.astype(jnp.bfloat16)
-        return carry
-
-    lax.fori_loop(0, TILES, tile_weights, 0)
+    def make_weights(some):
+        def tile_weights(j, carry):
+            start = pl.multiple_of(j * 128, 128)
+            log_norm = norm[pl.ds(j, 1), :]
+            ids = chosen[pl.ds(j, 1), :]
+            for place, lists, first in some:
+                soft = jnp.exp(logits[pl.ds(place, lists), pl.ds(start, 128)] - log_norm)
+                soft = jnp.where(sub[:lists] == ids - first, soft - 1.0, soft)
+                weights[pl.ds(place, lists), pl.ds(start, 128)] = soft.astype(jnp.bfloat16)
+            return carry
+
+        lax.fori_loop(0, TILES, tile_weights, 0)
 
     def pair_gradient(first, n):
         part[n, first * OWN : (first + 2) * OWN, :] = jnp.dot(
@@ -305,14 +322,17 @@
     def give_back(n):
         arrived(from_partner.at[n, 1], d_recv.at[n, 1])
         y_out[n] = part[n, 2 * OWN : 3 * OWN, :] + from_partner[n, 1]
-        to_owner.append(remote(y_out.at[n], y_in.at[n], y_send.at[n], y_recv.at[n], {"y": owner_y}))
-
+        for h, k in enumerate((-1, 1)):
+            source, target = y_out.at[n, pl.ds(h * HALF, HALF)], y_in.at[n, pl.ds(h * HALF, HALF)]
+            to_owner.append(remote(source, target, y_send.at[n, h], y_recv.at[n, h], {"y": at_y(k)}))
+
+    make_weights(parts[2:])
     for n in range(PARTS):
         pair_gradient(2, n)
         hand_over(n, 1)
-        if n:
-            give_back(n - 1)
-    give_back(PARTS - 1)
+    make_weights(parts[:2])
+    for n in range(PARTS):
+        give_back(n)
     wait2(loss2, h2_send, h2_recv)
     loss[0] = summed(loss2)
     loss_across = remote(loss.at[0], loss.at[1], l_send.at[0], l_recv.at[0], partner)
@@ -321,10 +341,11 @@
         hand_over(n, 0)
     loss_across.wait()
     loss[2] = loss[0] + loss[1]
-    loss_back = remote(loss.at[2], loss.at[3], l_send.at[1], l_recv.at[1], {"y": owner_y})
+    loss_back = remote(loss.at[2], loss.at[3], l_send.at[1], l_recv.at[1], {"y": at_y(1)})
     for n in range(PARTS):
         arrived(from_partner.at[n, 0], d_recv.at[n, 0])
-        arrived(y_in.at[n], y_recv.at[n])
+        for h in range(2):
+            arrived(y_in.at[n, pl.ds(h * HALF, HALF)], y_recv.at[n, h])
         grad_ref[:, n * WIDTH : (n + 1) * WIDTH] = part[n, :OWN, :] + from_partner[n, 0] + y_in[n]
     loss_back.wait()
     loss_ref[...] = jnp.sum(loss[2] + loss[3], keepdims=True) * (1.0 / ROWS)
@@ -349,7 +370,7 @@
             pltpu.VMEM((ROWS // 128, 128), i32),
             pltpu.VMEM((OWN, D), f32),
             pltpu.VMEM((TILES, 128), i32),
-            pltpu.VMEM((4, OWN, D), bf16),
+            pltpu.VMEM((HELD, D), bf16),
             pltpu.VMEM((HELD, DEV_ROWS), f32),
             pltpu.VMEM((HELD, DEV_ROWS), bf16),
             pltpu.VMEM((TILES, 128), f32),
@@ -363,9 +384,9 @@
             pltpu.VMEM((PARTS, 2, OWN, WIDTH), f32),
             pltpu.VMEM((PARTS, OWN, WIDTH), f32),
             pltpu.VMEM((PARTS, OWN, WIDTH), f32),
-            dma((PIECES + 2,)), dma((SENDS,)), dma((BLOCKS * PIECES,)), dma((3,)), dma((3,)),
+            dma((PIECES + 2,)), dma((SENDS,)), dma((BLOCKS * PIECES,)), dma((5,)), dma((5,)),
             dma((7,)), dma((8,)), dma((7,)), dma((8,)), dma((7,)), dma((8,)), dma((7,)), dma((8,)), dma((2,)), dma((2,)),
-            dma((PARTS, 2)), dma((PARTS, 2)), dma((PARTS,)), dma((PARTS,)),
+            dma((PARTS, 2)), dma((PARTS, 2)), dma((PARTS, 2)), dma((PARTS, 2)),
         ],
         compiler_params=pltpu.CompilerParams(collective_id=0, has_side_effects=True, vmem_limit_bytes=56000000),
     )(query_emb, positive_list.reshape(ROWS // 128, 128), centroids)

time: 62 us -> 58.5 us (0.944)
  Pallas kernels: 56.5 us -> 53 us
    pallas_call x1, Pallas kernels: 56.5 us -> 53 us  [shards(): pl.pallas_call(kernel, name='step', out_shape=(jax.ShapeDtypeStruct((OWN,...]
where the time goes in v3:
time: 58.5 us; the launch traced here: 58.3 us
  Pallas kernels  53 us (91%)
  between operations  2.41 us (4%)
  other arithmetic  2.13 us (4%)
  local copies, waits for them, and re-layouts  0.76 us (1%)
    pallas_call x1, Pallas kernels, shards(): pl.pallas_call(kernel, name='step', out_shape=(jax.ShapeDtypeStruct((OWN,...  53 us
    sub x1, other arithmetic, adam_update(): centroids - learn_rate * new_first / (jnp.sqrt(new_second) + epsilon)  2.13 us

profile of v3, /device:TPU:1, one launch (start us, length us, event | category | flops | bytes accessed | tf_op | source)
XLA Modules:
  0.0 58.3 jit_solution(17589301494130843090)
XLA Ops:
  0.6 0.0 copy-start
  0.6 0.7 %copy-done = s32[8192]{0:T(1024)S(1)} copy-done((s32[8192]{0:T(1024)S(1)}, s32[8192]{0:T(1024)}, u32[]{:S(2)}) %copy-start) | copy-done | bytes 32792
  1.4 0.0 copy-start.1
  1.4 0.0 copy-start.2
  1.4 53.0 %step.1 = (f32[128,768]{1,0:T(8,128)S(1)}, f32[1,1]{1,0:T(1,128)}) custom-call(bf16[256,768]{1,0:T(8,128)(2,1)} %query_hbm.1, s32[64,128]{1,0:T(8,128)S(1)} %bitcast.2, f32[128,768]{1,0:T(8,128)} %cent_hbm.1), custom_call_target="tpu_custom_call" | custom-call | tf_op jit(solution)/shard_map/step/pallas_call | solution.py:362
  54.4 0.0 copy-done.1
  54.4 0.0 copy-done.2
  54.4 2.1 %divide_subtract_fusion = (f32[128,768]{1,0:T(8,128)}, f32[128,768]{1,0:T(8,128)}, f32[128,768]{1,0:T(8,128)}) fusion(f32[128,768]{1,0:T(8,128)S(1)} %copy-done.1, f32[128,768]{1,0:T(8,128)S(1)} %get-tuple-element.6, f32[128,768]{1,0:T(8,128)S(1)} %copy-done.2, f32[128,768]{1,0:T(8,128)} %param.9), kind=kLoop, calls=%fused_computation.2 | loop fusion | flops 1081344 | bytes 2752512 | tf_op jit(solution)/shard_map/sub | solution.py:42
Async XLA Ops:
  0.6 0.8 %copy-start = (s32[8192]{0:T(1024)S(1)}, s32[8192]{0:T(1024)}, u32[]{:S(2)}) copy-start(s32[8192]{0:T(1024)} %param.6) | copy-start | bytes 98308
  1.4 53.0 %copy-start.1 = (f32[128,768]{1,0:T(8,128)S(1)}, f32[128,768]{1,0:T(8,128)}, u32[]{:S(2)}) copy-start(f32[128,768]{1,0:T(8,128)} %cent_hbm.1) | copy-start | bytes 1179652
  1.4 53.0 %copy-start.2 = (f32[128,768]{1,0:T(8,128)S(1)}, f32[128,768]{1,0:T(8,128)}, u32[]{:S(2)}) copy-start(f32[128,768]{1,0:T(8,128)} %param.8) | copy-start | bytes 1179652

commit v4 on v3

--- a/solution.py
+++ b/solution.py
@@ -53,45 +53,44 @@
     return top + jnp.log(total)
 
 
-STARTS = [('DURL', 'udLrRDU'), ('URDL', 'UDLR')]
-CUTS = ((16, 33, 41, 46, 51, 57, 61, 62), (20, 35, 39, 43, 47, 57, 61, 62))
-GROUPS = ((0, 1, -1, 2, -2, -3, 3, 4), (0, 1, -2, -1, 2, -3, 3, 4))
+STARTS = [('UDrRL', 'uDdLUR'), ('UDRL', 'UDLR')]
+CUTS = ((17, 31, 35, 46, 49, 51, 55, 62), (19, 29, 33, 47, 49, 52, 55, 62))
+GROUPS = ((0, -1, 1, 3, -2, 2, -3, 4), (0, -1, 1, -2, 2, -3, 3, 4))
 ROUTES = (
     (
-        (-1, 0, 0, "R"), (1, 0, 0, ""), (0, -1, 0, "uURL"), (0, 1, 0, "DRL"), (1, 0, 1, "U"), (2, 0, 1, "D"),
-        (0, -2, 1, "UrR"), (0, 2, 1, "LRD"), (-1, 0, 1, "UD"), (0, -1, 1, ""), (0, 1, 1, "L"), (2, 0, 0, "D"),
-        (1, -1, 0, ""), (0, 2, 0, "LDR"), (-1, -1, 0, "R"), (1, 1, 0, ""), (0, -3, 0, "RUL"), (-1, 1, 0, ""),
-        (0, -2, 0, "LR"), (1, 2, 1, "D"), (2, 1, 1, "D"), (1, -1, 1, "UL"), (1, 1, 1, ""), (0, 3, 1, ""),
-        (0, -3, 1, "UR"), (2, -2, 1, "U"), (-1, -2, 1, ""), (1, 2, 0, "L"), (-1, 1, 1, ""), (-1, -1, 1, ""),
-        (-1, 2, 1, "D"), (1, -3, 0, "U"), (2, 1, 0, ""), (0, 4, 0, "r"), (-1, 2, 0, ""), (2, -1, 0, ""),
-        (1, -2, 0, "L"), (0, 3, 0, "RL"), (1, -2, 1, "U"), (-1, -3, 0, "UR"), (2, -1, 1, ""), (1, 3, 1, "DL"),
-        (0, 4, 1, "R"), (-1, -2, 0, ""), (2, 2, 0, "D"), (2, 2, 1, ""), (2, -3, 1, "U"), (-1, -3, 1, ""),
-        (-1, 3, 1, ""), (1, 4, 0, ""), (2, -2, 0, ""), (1, -3, 1, ""), (2, 4, 0, ""), (-1, 3, 0, ""), (1, 3, 0, ""),
-        (1, 4, 1, ""), (2, -3, 0, ""), (-1, 4, 0, ""), (2, 3, 1, ""), (2, 3, 0, ""), (-1, 4, 1, ""), (2, 4, 1, ""),
+        (0, -1, 0, "UL"), (0, 1, 0, "DRL"), (1, 0, 1, "LU"), (0, 1, 1, "RL"), (2, 0, 0, "D"), (-1, 0, 0, "U"),
+        (0, -2, 1, "RUL"), (0, -1, 1, "R"), (0, 2, 1, "DL"), (0, -2, 0, "RU"), (1, -1, 0, "UL"), (0, 2, 0, "DRL"),
+        (-1, 1, 1, "DR"), (2, 1, 0, "d"), (2, 0, 1, "U"), (1, 0, 0, ""), (-1, 0, 1, ""), (-1, -2, 1, "U"),
+        (0, 3, 1, "rRD"), (0, -3, 1, "L"), (0, 3, 0, "DL"), (-1, -2, 0, "UR"), (1, 2, 1, "D"), (-1, 2, 1, "R"),
+        (1, -2, 0, "U"), (-1, 2, 0, "D"), (2, -1, 1, "U"), (1, -1, 1, ""), (-1, -1, 0, ""), (-1, -1, 1, ""),
+        (2, -1, 0, ""), (-1, 1, 0, ""), (1, 1, 0, ""), (1, 1, 1, ""), (2, 1, 1, ""), (1, 2, 0, "L"), (2, 3, 0, "D"),
+        (-1, -3, 1, "U"), (1, -3, 1, "UL"), (-1, -3, 0, "R"), (0, 4, 0, "RL"), (2, 3, 1, "D"), (-1, 3, 1, ""),
+        (1, 3, 0, ""), (1, 3, 1, ""), (-1, 3, 0, ""), (1, -2, 1, ""), (2, -2, 0, ""), (2, -2, 1, ""), (2, 2, 1, ""),
+        (2, 2, 0, ""), (0, -3, 0, ""), (1, -3, 0, ""), (2, -3, 1, ""), (2, -3, 0, ""), (0, 4, 1, ""), (2, 4, 0, ""),
+        (-1, 4, 1, ""), (1, 4, 0, ""), (2, 4, 1, ""), (-1, 4, 0, ""), (1, 4, 1, ""),
     ),
     (
-        (-1, 0, 0, "D"), (1, 0, 0, "L"), (0, -1, 0, "URL"), (0, 1, 0, "DL"), (-1, 0, 1, "D"), (1, 0, 1, "DL"),
-        (0, -1, 1, "RUL"), (0, 1, 1, "D"), (2, 0, 0, "D"), (-1, -1, 0, "R"), (0, -2, 0, "UR"), (-1, 1, 0, "D"),
-        (1, -1, 0, "U"), (0, 2, 0, "LD"), (-1, -1, 1, "U"), (0, -2, 1, "UL"), (-1, 1, 1, ""), (1, 1, 0, ""),
-        (1, 1, 1, "DL"), (2, 0, 1, ""), (2, -1, 0, "U"), (0, -3, 0, "LU"), (0, 2, 1, "RD"), (1, -1, 1, "L"),
-        (-1, -2, 0, "U"), (1, -2, 0, ""), (2, 1, 0, ""), (1, 2, 0, "DL"), (-1, -2, 1, "RU"), (-1, 2, 0, "D"),
-        (1, -2, 1, ""), (0, -3, 1, "UL"), (-1, 2, 1, "DR"), (0, 3, 0, ""), (2, 1, 1, ""), (2, -2, 0, ""),
-        (1, 2, 1, "D"), (1, -3, 0, "L"), (2, -2, 1, "u"), (0, 4, 0, "RL"), (0, 3, 1, ""), (2, -1, 1, ""),
-        (-1, -3, 0, ""), (2, 2, 1, "D"), (1, 3, 0, ""), (2, 2, 0, ""), (-1, -3, 1, ""), (-1, 3, 0, "R"),
-        (1, -3, 1, "L"), (-1, 3, 1, "D"), (-1, 4, 0, ""), (0, 4, 1, "L"), (2, -3, 0, "U"), (1, 3, 1, ""),
-        (1, 4, 0, ""), (2, 3, 1, ""), (2, -3, 1, ""), (2, 3, 0, ""), (-1, 4, 1, ""), (2, 4, 1, ""), (1, 4, 1, ""),
-        (2, 4, 0, ""),
+        (-1, 0, 0, "DR"), (1, 0, 0, "d"), (0, -1, 0, "LUR"), (0, 1, 0, "DL"), (-1, 0, 1, "DR"), (1, 0, 1, "D"),
+        (0, -1, 1, "uRLU"), (0, 1, 1, "D"), (1, -1, 0, "uL"), (0, -2, 0, "RUL"), (-1, 1, 0, "R"), (1, -1, 1, "U"),
+        (1, 2, 0, "L"), (0, 2, 0, "RD"), (0, -3, 1, "L"), (-1, -1, 1, "UR"), (-1, -2, 0, "UR"), (2, 0, 0, ""),
+        (2, 0, 1, ""), (1, 1, 1, "L"), (0, 2, 1, "DRL"), (1, -3, 0, "LU"), (-1, 2, 0, "D"), (1, -3, 1, "UL"),
+        (0, -3, 0, "U"), (0, 3, 0, "L"), (-1, -1, 0, ""), (2, -1, 0, ""), (2, -1, 1, ""), (1, 1, 0, ""),
+        (-1, 1, 1, ""), (2, 1, 0, ""), (2, 1, 1, ""), (1, -2, 1, "L"), (1, 2, 1, "D"), (0, 3, 1, "RD"),
+        (-1, -2, 1, "U"), (-1, 2, 1, "R"), (2, -3, 0, "U"), (-1, 3, 0, "D"), (1, 3, 0, "L"), (-1, 3, 1, "DR"),
+        (1, 4, 1, "L"), (0, -2, 1, ""), (1, -2, 0, ""), (2, -2, 0, ""), (2, -2, 1, ""), (2, 2, 0, ""), (2, 2, 1, ""),
+        (-1, -3, 0, ""), (2, -3, 1, ""), (-1, -3, 1, ""), (1, 3, 1, ""), (2, 3, 0, ""), (2, 3, 1, ""), (1, 4, 0, ""),
+        (0, 4, 1, ""), (0, 4, 0, ""), (-1, 4, 0, ""), (-1, 4, 1, ""), (2, 4, 0, ""), (2, 4, 1, ""),
     ),
 )
 
 
 def kernel(
-    query_hbm, pos_hbm, cent_hbm, grad_ref, loss_ref,
+    query_hbm, pos_hbm, cent_hbm, grad_hbm, loss_ref,
     q, pos, cent, chosen, table, logits, weights, norm, hit, stat1, stat2, hit1, loss2, loss,
-    part, from_partner, y_out, y_in,
+    part, from_partner, y_out, y_in, grad,
     own_sem, q_send, q_recv, t_send, t_recv,
     s1_send, s1_recv, s2_send, s2_recv, h1_send, h1_recv, h2_send, h2_recv, l_send, l_recv,
-    d_send, d_recv, y_send, y_recv,
+    d_send, d_recv, y_send, y_recv, g_sem,
 ):
     x, z, y, c = (lax.axis_index(a) for a in AXES)
 
@@ -107,9 +106,10 @@
     other = 1 - c
     partner = {"c": other}
 
-    group1 = [(dx, dy) for dy in (0, 2) for dx in range(NX) if (dx, dy) != (0, 0)]
+    group1 = [(2, 2), (1, 2), (3, 2), (0, 2), (2, 0), (1, 0), (3, 0)]
     peers = [{"x": at_x(k)} for k in (1, -1, 2)] + [{"z": at_z(k)} for k in (1, -1, 2, -2)]
     peers += [partner] + [{"y": at_y(k), "c": core} for k in (1, -1) for core in (c, other)]
+    group2 = (4, 3, 5, 2, 6, 1, 7)
     barrier = pltpu.get_barrier_semaphore()
     for peer in peers:
         pl.semaphore_signal(barrier, inc=1, device_id=peer, device_id_type=MESH)
@@ -151,9 +151,7 @@
         def send(dx, dz, p, links):
             place = at_z(dz) * NX + at_x(dx)
             for link in links:
-                remote(
-                    q.at[place, p], q.at[place, p], q_send.at[count[0]], q_recv.at[place * PIECES + p], toward[link]
-                )
+                remote(q.at[place, p], q.at[place, p], q_send.at[count[0]], q_recv.at[place * PIECES + p], toward[link])
                 count[0] += 1
 
         return send, count
@@ -257,19 +255,17 @@
             remote(slots.at[me1], slots.at[me1], send.at[k], recv.at[me1], {"x": at_x(dx), "y": at_y(dy)})
 
     def wait1(slots, send, recv):
-        for k, (dx, dy) in enumerate(group1):
+        for dx, dy in group1:
             place = lax.div(at_y(dy), 2) * NX + at_x(dx)
             arrived(slots.at[place], recv.at[place])
-            arrived(slots.at[0], send.at[k])
 
     def exchange2(slots, send, recv):
-        for dz in range(1, NZ):
-            remote(slots.at[z], slots.at[z], send.at[dz - 1], recv.at[z], {"z": at_z(dz)})
+        for k, dz in enumerate(group2):
+            remote(slots.at[z], slots.at[z], send.at[k], recv.at[z], {"z": at_z(dz)})
 
     def wait2(slots, send, recv):
-        for dz in range(1, NZ):
+        for dz in group2:
             arrived(slots.at[at_z(dz)], recv.at[at_z(dz)])
-            arrived(slots.at[0], send.at[dz - 1])
 
     def summed(slots):
         total = slots[0]
@@ -313,7 +309,7 @@
             preferred_element_type=jnp.float32,
         )
 
-    to_partner, to_owner = [], []
+    to_partner, to_owner, outs = [], [], []
 
     def hand_over(n, slot):
         lists = part.at[n, pl.ds((1 + 2 * slot) * OWN, OWN)]
@@ -346,14 +342,22 @@
         arrived(from_partner.at[n, 0], d_recv.at[n, 0])
         for h in range(2):
             arrived(y_in.at[n, pl.ds(h * HALF, HALF)], y_recv.at[n, h])
-        grad_ref[:, n * WIDTH : (n + 1) * WIDTH] = part[n, :OWN, :] + from_partner[n, 0] + y_in[n]
+        grad[n] = part[n, :OWN, :] + from_partner[n, 0] + y_in[n]
+        out = pltpu.make_async_copy(grad.at[n], grad_hbm.at[:, pl.ds(n * WIDTH, WIDTH)], g_sem.at[n])
+        out.start()
+        outs.append(out)
     loss_back.wait()
     loss_ref[...] = jnp.sum(loss[2] + loss[3], keepdims=True) * (1.0 / ROWS)
 
     for k in range(SENDS):
         arrived(q.at[0, 0], q_send.at[k])
+    for slots, send in ((stat1, s1_send), (hit1, h1_send), (stat2, s2_send), (loss2, h2_send)):
+        for k in range(7):
+            arrived(slots.at[0], send.at[k])
     for copy in table_sends + to_partner + to_owner:
         copy.wait_send()
+    for copy in outs:
+        copy.wait()
 
 
 def shards(query_emb, positive_list, centroids, first_moment, second_moment):
@@ -364,7 +368,7 @@
         name="step",
         out_shape=(jax.ShapeDtypeStruct((OWN, D), f32), jax.ShapeDtypeStruct((1, 1), f32)),
         in_specs=[hbm, hbm, hbm],
-        out_specs=(vmem, vmem),
+        out_specs=(hbm, vmem),
         scratch_shapes=[
             pltpu.VMEM((BLOCKS, PIECES, PIECE, D), bf16),
             pltpu.VMEM((ROWS // 128, 128), i32),
@@ -384,11 +388,12 @@
             pltpu.VMEM((PARTS, 2, OWN, WIDTH), f32),
             pltpu.VMEM((PARTS, OWN, WIDTH), f32),
             pltpu.VMEM((PARTS, OWN, WIDTH), f32),
+            pltpu.VMEM((PARTS, OWN, WIDTH), f32),
             dma((PIECES + 2,)), dma((SENDS,)), dma((BLOCKS * PIECES,)), dma((5,)), dma((5,)),
             dma((7,)), dma((8,)), dma((7,)), dma((8,)), dma((7,)), dma((8,)), dma((7,)), dma((8,)), dma((2,)), dma((2,)),
-            dma((PARTS, 2)), dma((PARTS, 2)), dma((PARTS, 2)), dma((PARTS, 2)),
+            dma((PARTS, 2)), dma((PARTS, 2)), dma((PARTS, 2)), dma((PARTS, 2)), dma((PARTS,)),
         ],
-        compiler_params=pltpu.CompilerParams(collective_id=0, has_side_effects=True, vmem_limit_bytes=56000000),
+        compiler_params=pltpu.CompilerParams(collective_id=0, has_side_effects=True, vmem_limit_bytes=65800000),
     )(query_emb, positive_list.reshape(ROWS // 128, 128), centroids)
     return (*adam_update(centroids, first_moment, second_moment, gradient), loss[0, 0])
 

time: 58.5 us -> 57.6 us (0.985)
  local copies, waits for them, and re-layouts: 0.76 us -> 0.01 us
    unnamed x6 -> x4, local copies, waits for them, and re-layouts: 0.76 us -> 0.01 us
where the time goes in v4:
time: 57.6 us; the launch traced here: 57.5 us
  Pallas kernels  52.7 us (91%)
  between operations  2.47 us (4%)
  other arithmetic  2.25 us (4%)
    pallas_call x1, Pallas kernels, shards(): pl.pallas_call(kernel, name='step', out_shape=(jax.ShapeDtypeStruct((OWN,...  52.7 us
    sub x1, other arithmetic, adam_update(): centroids - learn_rate * new_first / (jnp.sqrt(new_second) + epsilon)  2.25 us

profile of v4, /device:TPU:1, one launch (start us, length us, event | category | flops | bytes accessed | tf_op | source)
XLA Modules:
  0.0 57.5 jit_solution(4497761421139126746)
XLA Ops:
  0.6 0.0 copy-start
  0.6 0.0 copy-start.1
  0.7 52.7 %step.1 = (f32[128,768]{1,0:T(8,128)}, f32[1,1]{1,0:T(1,128)}) custom-call(bf16[256,768]{1,0:T(8,128)(2,1)} %query_hbm.1, s32[64,128]{1,0:T(8,128)} %bitcast.2, f32[128,768]{1,0:T(8,128)} %cent_hbm.1), custom_call_target="tpu_custom_call" | custom-call | tf_op jit(solution)/shard_map/step/pallas_call | solution.py:366
  53.4 0.0 copy-done
  53.4 0.0 copy-done.1
  53.4 2.2 %divide_subtract_fusion = (f32[128,768]{1,0:T(8,128)}, f32[128,768]{1,0:T(8,128)}, f32[128,768]{1,0:T(8,128)}) fusion(f32[128,768]{1,0:T(8,128)S(1)} %copy-done, f32[128,768]{1,0:T(8,128)} %get-tuple-element.6, f32[128,768]{1,0:T(8,128)S(1)} %copy-done.1, f32[128,768]{1,0:T(8,128)} %param.9), kind=kLoop, calls=%fused_computation.2 | loop fusion | flops 1081344 | bytes 2752512 | tf_op jit(solution)/shard_map/sub | solution.py:42
Async XLA Ops:
  0.6 52.8 %copy-start = (f32[128,768]{1,0:T(8,128)S(1)}, f32[128,768]{1,0:T(8,128)}, u32[]{:S(2)}) copy-start(f32[128,768]{1,0:T(8,128)} %cent_hbm.1) | copy-start | bytes 1179652
  0.6 52.8 %copy-start.1 = (f32[128,768]{1,0:T(8,128)S(1)}, f32[128,768]{1,0:T(8,128)}, u32[]{:S(2)}) copy-start(f32[128,768]{1,0:T(8,128)} %param.8) | copy-start | bytes 1179652

commit v5 on v4

--- a/solution.py
+++ b/solution.py
@@ -53,33 +53,33 @@
     return top + jnp.log(total)
 
 
-STARTS = [('UDrRL', 'uDdLUR'), ('UDRL', 'UDLR')]
-CUTS = ((17, 31, 35, 46, 49, 51, 55, 62), (19, 29, 33, 47, 49, 52, 55, 62))
-GROUPS = ((0, -1, 1, 3, -2, 2, -3, 4), (0, -1, 1, -2, 2, -3, 3, 4))
+STARTS = [('UDLR', 'RuUdDrL'), ('UDRL', 'UDLR')]
+CUTS = ((17, 30, 41, 45, 48, 53, 57, 62), (18, 26, 32, 42, 49, 52, 56, 62))
+GROUPS = ((0, 1, 2, -1, -2, 3, -3, 4), (0, -1, 1, -2, 2, -3, 3, 4))
 ROUTES = (
     (
-        (0, -1, 0, "UL"), (0, 1, 0, "DRL"), (1, 0, 1, "LU"), (0, 1, 1, "RL"), (2, 0, 0, "D"), (-1, 0, 0, "U"),
-        (0, -2, 1, "RUL"), (0, -1, 1, "R"), (0, 2, 1, "DL"), (0, -2, 0, "RU"), (1, -1, 0, "UL"), (0, 2, 0, "DRL"),
-        (-1, 1, 1, "DR"), (2, 1, 0, "d"), (2, 0, 1, "U"), (1, 0, 0, ""), (-1, 0, 1, ""), (-1, -2, 1, "U"),
-        (0, 3, 1, "rRD"), (0, -3, 1, "L"), (0, 3, 0, "DL"), (-1, -2, 0, "UR"), (1, 2, 1, "D"), (-1, 2, 1, "R"),
-        (1, -2, 0, "U"), (-1, 2, 0, "D"), (2, -1, 1, "U"), (1, -1, 1, ""), (-1, -1, 0, ""), (-1, -1, 1, ""),
-        (2, -1, 0, ""), (-1, 1, 0, ""), (1, 1, 0, ""), (1, 1, 1, ""), (2, 1, 1, ""), (1, 2, 0, "L"), (2, 3, 0, "D"),
-        (-1, -3, 1, "U"), (1, -3, 1, "UL"), (-1, -3, 0, "R"), (0, 4, 0, "RL"), (2, 3, 1, "D"), (-1, 3, 1, ""),
-        (1, 3, 0, ""), (1, 3, 1, ""), (-1, 3, 0, ""), (1, -2, 1, ""), (2, -2, 0, ""), (2, -2, 1, ""), (2, 2, 1, ""),
-        (2, 2, 0, ""), (0, -3, 0, ""), (1, -3, 0, ""), (2, -3, 1, ""), (2, -3, 0, ""), (0, 4, 1, ""), (2, 4, 0, ""),
-        (-1, 4, 1, ""), (1, 4, 0, ""), (2, 4, 1, ""), (-1, 4, 0, ""), (1, 4, 1, ""),
+        (1, 0, 0, "DL"), (0, -1, 0, "uURL"), (0, 1, 0, "DrR"), (-1, 0, 1, "D"), (0, -2, 1, "ULr"), (0, 2, 1, "DL"),
+        (0, -1, 1, "RL"), (0, 1, 1, "L"), (2, 0, 1, "D"), (2, 0, 0, "U"), (1, 1, 0, "D"), (0, 2, 0, "D"),
+        (0, -3, 0, "RUL"), (0, -2, 0, "RL"), (-1, 1, 1, "D"), (-1, 0, 0, ""), (1, 0, 1, ""), (2, 1, 0, "D"),
+        (1, -2, 1, "U"), (-1, 1, 0, "D"), (0, -3, 1, "U"), (0, 3, 1, "r"), (1, 2, 1, "DL"), (-1, -1, 1, "U"),
+        (1, -1, 1, "L"), (1, 2, 0, "D"), (-1, -3, 0, "UR"), (0, 4, 0, "L"), (2, 1, 1, ""), (1, 1, 1, ""),
+        (0, 3, 0, "R"), (-1, -2, 0, "R"), (1, -3, 1, "UL"), (-1, 2, 1, "D"), (0, 4, 1, "R"), (2, 2, 0, "D"),
+        (-1, -2, 1, "U"), (2, 3, 1, "D"), (-1, 4, 0, "R"), (2, 2, 1, ""), (-1, 2, 0, ""), (-1, -1, 0, ""),
+        (1, -1, 0, ""), (2, -1, 0, ""), (2, -1, 1, ""), (2, -2, 1, ""), (1, -2, 0, ""), (2, -2, 0, ""),
+        (1, 3, 1, ""), (-1, 3, 0, ""), (1, 3, 0, ""), (-1, 3, 1, ""), (2, 3, 0, ""), (1, -3, 0, ""), (2, -3, 0, ""),
+        (2, -3, 1, ""), (-1, -3, 1, ""), (1, 4, 1, ""), (1, 4, 0, ""), (-1, 4, 1, ""), (2, 4, 1, ""), (2, 4, 0, ""),
     ),
     (
-        (-1, 0, 0, "DR"), (1, 0, 0, "d"), (0, -1, 0, "LUR"), (0, 1, 0, "DL"), (-1, 0, 1, "DR"), (1, 0, 1, "D"),
-        (0, -1, 1, "uRLU"), (0, 1, 1, "D"), (1, -1, 0, "uL"), (0, -2, 0, "RUL"), (-1, 1, 0, "R"), (1, -1, 1, "U"),
-        (1, 2, 0, "L"), (0, 2, 0, "RD"), (0, -3, 1, "L"), (-1, -1, 1, "UR"), (-1, -2, 0, "UR"), (2, 0, 0, ""),
-        (2, 0, 1, ""), (1, 1, 1, "L"), (0, 2, 1, "DRL"), (1, -3, 0, "LU"), (-1, 2, 0, "D"), (1, -3, 1, "UL"),
-        (0, -3, 0, "U"), (0, 3, 0, "L"), (-1, -1, 0, ""), (2, -1, 0, ""), (2, -1, 1, ""), (1, 1, 0, ""),
-        (-1, 1, 1, ""), (2, 1, 0, ""), (2, 1, 1, ""), (1, -2, 1, "L"), (1, 2, 1, "D"), (0, 3, 1, "RD"),
-        (-1, -2, 1, "U"), (-1, 2, 1, "R"), (2, -3, 0, "U"), (-1, 3, 0, "D"), (1, 3, 0, "L"), (-1, 3, 1, "DR"),
-        (1, 4, 1, "L"), (0, -2, 1, ""), (1, -2, 0, ""), (2, -2, 0, ""), (2, -2, 1, ""), (2, 2, 0, ""), (2, 2, 1, ""),
-        (-1, -3, 0, ""), (2, -3, 1, ""), (-1, -3, 1, ""), (1, 3, 1, ""), (2, 3, 0, ""), (2, 3, 1, ""), (1, 4, 0, ""),
-        (0, 4, 1, ""), (0, 4, 0, ""), (-1, 4, 0, ""), (-1, 4, 1, ""), (2, 4, 0, ""), (2, 4, 1, ""),
+        (-1, 0, 0, "DR"), (0, -1, 0, "RUL"), (0, 1, 0, "DL"), (-1, 0, 1, "D"), (1, 0, 1, "UL"), (0, -1, 1, "UR"),
+        (0, 1, 1, "DL"), (2, 0, 0, "U"), (0, -2, 0, "UL"), (-1, 1, 0, "D"), (-1, -1, 0, "U"), (1, 1, 0, "DL"),
+        (0, 2, 0, "D"), (1, -1, 1, "uL"), (2, 0, 1, "D"), (0, -2, 1, "URL"), (0, 2, 1, "RDL"), (1, 0, 0, ""),
+        (-1, 2, 0, "R"), (0, -3, 0, "L"), (-1, -2, 0, "UR"), (-1, -2, 1, "R"), (1, -1, 0, ""), (-1, -1, 1, ""),
+        (2, -1, 0, ""), (2, -1, 1, ""), (0, 3, 0, "DLR"), (-1, 2, 1, "D"), (2, 1, 1, "D"), (-1, 1, 1, ""),
+        (1, 1, 1, ""), (2, 1, 0, ""), (1, -3, 1, "LU"), (0, 3, 1, "L"), (0, -3, 1, "UR"), (2, -2, 0, "u"),
+        (1, -3, 0, "L"), (0, 4, 0, "L"), (-1, -3, 0, "U"), (1, -2, 0, ""), (1, -2, 1, ""), (2, -2, 1, ""),
+        (1, 3, 0, "L"), (-1, 3, 1, "R"), (2, -3, 1, "U"), (1, 2, 0, ""), (2, 2, 0, ""), (1, 2, 1, ""), (2, 2, 1, ""),
+        (0, 4, 1, "R"), (-1, -3, 1, ""), (2, -3, 0, ""), (-1, 3, 0, ""), (1, 3, 1, ""), (2, 3, 1, ""), (2, 3, 0, ""),
+        (1, 4, 1, ""), (1, 4, 0, ""), (2, 4, 0, ""), (-1, 4, 0, ""), (2, 4, 1, ""), (-1, 4, 1, ""),
     ),
 )
 

time: 57.6 us -> 57.2 us (level)
  no operation moved by 1% of the time
where the time goes in v5:
time: 57.2 us; the launch traced here: 57.1 us
  Pallas kernels  52.3 us (91%)
  between operations  2.47 us (4%)
  other arithmetic  2.25 us (4%)
    pallas_call x1, Pallas kernels, shards(): pl.pallas_call(kernel, name='step', out_shape=(jax.ShapeDtypeStruct((OWN,...  52.3 us
    sub x1, other arithmetic, adam_update(): centroids - learn_rate * new_first / (jnp.sqrt(new_second) + epsilon)  2.25 us

profile of v5, /device:TPU:1, one launch (start us, length us, event | category | flops | bytes accessed | tf_op | source)
XLA Modules:
  0.0 57.1 jit_solution(8206114765486054633)
XLA Ops:
  0.6 0.0 copy-start
  0.6 0.0 copy-start.1
  0.7 52.3 %step.1 = (f32[128,768]{1,0:T(8,128)}, f32[1,1]{1,0:T(1,128)}) custom-call(bf16[256,768]{1,0:T(8,128)(2,1)} %query_hbm.1, s32[64,128]{1,0:T(8,128)} %bitcast.2, f32[128,768]{1,0:T(8,128)} %cent_hbm.1), custom_call_target="tpu_custom_call" | custom-call | tf_op jit(solution)/shard_map/step/pallas_call | solution.py:366
  53.0 0.0 copy-done
  53.0 0.0 copy-done.1
  53.0 2.2 %divide_subtract_fusion = (f32[128,768]{1,0:T(8,128)}, f32[128,768]{1,0:T(8,128)}, f32[128,768]{1,0:T(8,128)}) fusion(f32[128,768]{1,0:T(8,128)S(1)} %copy-done, f32[128,768]{1,0:T(8,128)} %get-tuple-element.6, f32[128,768]{1,0:T(8,128)S(1)} %copy-done.1, f32[128,768]{1,0:T(8,128)} %param.9), kind=kLoop, calls=%fused_computation.2 | loop fusion | flops 1081344 | bytes 2752512 | tf_op jit(solution)/shard_map/sub | solution.py:42
Async XLA Ops:
  0.6 52.4 %copy-start = (f32[128,768]{1,0:T(8,128)S(1)}, f32[128,768]{1,0:T(8,128)}, u32[]{:S(2)}) copy-start(f32[128,768]{1,0:T(8,128)} %cent_hbm.1) | copy-start | bytes 1179652
  0.6 52.4 %copy-start.1 = (f32[128,768]{1,0:T(8,128)S(1)}, f32[128,768]{1,0:T(8,128)}, u32[]{:S(2)}) copy-start(f32[128,768]{1,0:T(8,128)} %param.8) | copy-start | bytes 1179652
